TPU v7x, 256 devices: a whole 4x4x8 slice. The times are simulated.
256 devices in a mesh: seg: 8 (over x_hi, y), lat: 32 (over z, x_lo, core).
Axes of the slice: x: 4 (x_hi: 2, x_lo: 2; x = x_hi * 2 + x_lo), y: 4, z: 8, core: 2. Of those that a mesh axis runs over, the one named last changes fastest.
Arguments:
- coh_map: bfloat16 [8, 65536, 128], P('seg', 'lat'), may hold values from 0 to 40, as said below
- positions: int32 [8, 4096], P('seg', 'lat'), may hold values from 0 to 16776959, as said below
- counts: int32 [64], P('lat'), may hold values from 1 to 64, as said below
Outputs:
- semi_stat: bfloat16 [4096, 128], P('lat')
- excess: float32 [64, 128], P('lat')
Inputs may be any that keep to these rules, and one draw needn't show every extreme that they name: `coh_map`: nonnegative. `counts`: the first block has 1 valid point and the last block 64. `positions`: the bins are split into 32 aligned slices of 2048 bins; a point's two bins lie in the same slice; in each segment, at most 8 of the 128 points of one index of lat have their bins in one slice, and that most is reached in every draw.
All inputs are finite; a program needn't handle non-finite values.
Results may differ from a plain program's by a relative error of at most 0.001.
Values sent between devices are 32-bit elements; how exact they have to be, the bound alone decides.
A program may use at most 64 MiB of HBM per device.

v0:
```python
import jax
import jax.numpy as jnp
from jax import lax
from jax.sharding import PartitionSpec as P


def copy_for_each(shard, axis):
    copies = jnp.broadcast_to(shard, (lax.axis_size(axis), *shard.shape))
    return lax.all_to_all(copies, axis, split_axis=0, concat_axis=0, tiled=True)


def of_everyone(shard, axis):
    everything = copy_for_each(shard, axis)
    return jnp.sum(everything, axis=0)


def packed_total(arrays, axis):
    ends = [0]
    for a in arrays:
        ends.append(ends[-1] + a.size)
    subtotal = of_everyone(jnp.concatenate([a.ravel() for a in arrays]), axis)
    return tuple((subtotal[b:e].reshape(a.shape) for a, b, e in zip(arrays, ends, ends[1:])))


def routed_sums(positions, coh_map, first_bin):
    seg_count = coh_map.shape[0]
    slice_bins = coh_map.shape[1]
    width = coh_map.shape[2]
    own_rows = positions.shape[1]
    n_lataxis = lax.axis_size("lat")
    slot_limit = 2 * own_rows // n_lataxis
    dest = positions // 256 // slice_bins
    dest_hits = (dest[:, :, None] == lax.broadcasted_iota(jnp.int32, (1, 1, n_lataxis), 2)).astype(
        jnp.int32
    )
    before = jnp.cumsum(dest_hits, axis=1) - dest_hits
    slot = jnp.sum(before * dest_hits, axis=2)
    seg_ids = lax.broadcasted_iota(jnp.int32, positions.shape, 0)
    outgoing = (
        jnp.full((n_lataxis, seg_count, slot_limit), -1, jnp.int32)
        .at[dest, seg_ids, slot]
        .set(positions)
    )
    bin_index = lax.broadcasted_iota(jnp.int32, (1, slice_bins), 1)
    incoming = lax.all_to_all(outgoing, "lat", split_axis=0, concat_axis=0, tiled=True)
    item_count = incoming.shape[2]
    pos_flat = incoming[:, 0, :].reshape(-1)
    live = (pos_flat >= 0)[:, None]
    rel_bin = (pos_flat // 256 - first_bin)[:, None]
    fraction = (pos_flat % 256).astype(jnp.float32)[:, None] / 256.0
    weights = jnp.where(live & (bin_index == rel_bin), 1.0 - fraction, 0.0) + jnp.where(
        live & (bin_index == rel_bin + 1), fraction, 0.0
    )
    rows = jnp.dot(weights.astype(jnp.bfloat16), coh_map[0], preferred_element_type=jnp.float32)
    row_list = [rows.reshape(n_lataxis, item_count, width)]
    stacked = jnp.stack(row_list, axis=1)
    returned = lax.all_to_all(stacked, "lat", split_axis=0, concat_axis=0, tiled=True)
    by_segment = returned.transpose(1, 0, 2, 3).reshape(seg_count, n_lataxis * slot_limit, width)
    flat_index = dest * slot_limit + slot
    picked = jnp.take_along_axis(by_segment, flat_index[:, :, None], axis=1)
    return jnp.sum(picked, axis=0)


def shards(coh_map, positions, counts):
    seg_count = coh_map.shape[0]
    slice_bins = coh_map.shape[1]
    first_bin = lax.axis_index("lat") * slice_bins
    n_segaxis = lax.axis_size("seg")
    total_segs = seg_count * n_segaxis
    own_rows = positions.shape[1]
    local_sums_rows = routed_sums(positions, coh_map, first_bin)
    summed = of_everyone(local_sums_rows, "seg")
    semi_stat = summed / total_segs
    block_count = counts.shape[0]
    block_size = own_rows // block_count
    grouped = semi_stat.reshape(block_count, block_size, semi_stat.shape[1])
    slot_index = lax.broadcasted_iota(jnp.int32, (block_count, block_size, 1), 1)
    live_mask = slot_index < counts[:, None, None]
    block_sums = jnp.sum(jnp.where(live_mask, grouped, 0.0), axis=1)
    count_float = counts.astype(jnp.float32)
    block_means = block_sums / count_float[:, None]
    column_sums, total_count = packed_total(
        (jnp.sum(block_sums, axis=0), jnp.sum(count_float)), "lat"
    )
    global_mean = column_sums / total_count
    excess = block_means - global_mean[None, :]
    return (semi_stat.astype(jnp.bfloat16), excess)


def solution(mesh):
    in_specs = (P("seg", "lat", None), P("seg", "lat"), P("lat"))
    out_specs = (P("lat", None), P("lat", None))
    return jax.shard_map(shards, mesh=mesh, in_specs=in_specs, out_specs=out_specs, check_vma=False)
```

profile of v0, /device:TPU:1, one launch (start us, length us, event | category | flops | bytes accessed | tf_op | source)
XLA Modules:
  0.0 83.6 jit_solution(5213367111190894485)
XLA Ops:
  0.6 0.7 fusion.19
  1.5 0.2 reduce_window_sum.11
  1.6 0.2 select_reduce_fusion.2
  1.9 10.9 %scatter_fusion = s32[32,8]{0,1:T(8,128)S(1)} fusion(s32[32,8]{0,1:T(8,128)S(1)} %broadcast.431, s32[128]{0:T(128)S(1)} %fusion.21, s32[128]{0:T(128)} %bitcast.72), kind=kCustom, calls=%fused_computation.1 | custom fusion | bytes 2560 | tf_op jit(solution)/shard_map/scatter | solution.py:42
  12.8 0.7 copy.26
  13.5 11.0 %all-to-all-start = ((s32[32,1,8]{2,1,0:T(1,128)}), s32[32,1,8]{2,1,0:T(1,128)S(1)}, u32[]{:S(2)}, u32[]{:S(2)}) async-start(s32[32,1,8]{2,1,0:T(1,128)} %copy.26), calls=%async_computation | async-start | bytes 32768 | tf_op jit(solution)/shard_map/all_to_all | solution.py:45
  24.6 7.8 %all-to-all-done = s32[32,1,8]{2,1,0:T(1,128)S(1)} async-done(((s32[32,1,8]{2,1,0:T(1,128)}), s32[32,1,8]{2,1,0:T(1,128)S(1)}, u32[]{:S(2)}, u32[]{:S(2)}) %all-to-all-start) | async-done | bytes 1056 | tf_op jit(solution)/shard_map/all_to_all | solution.py:45
  32.9 1.7 %convolution_bitcast_fusion = f32[32,1,8,128]{3,2,1,0:T(8,128)} fusion(f32[32,8]{1,0:T(8,128)S(1)} %copy.32, s32[32,8]{1,0:T(8,128)S(1)} %copy.31, f32[32,8]{1,0:T(8,128)S(1)} %copy.30, s32[32,8]{1,0:T(8,128)S(1)} %copy.29, pred[32,8]{1,0:T(8,128)(4,1)S(1)} %copy.28, bf16[1,2048,128]{2,1,0:T(8,128)(2,1)S(1)} %copy-done), kind=kOutput, calls=%fused_computation.7 | convolution fusion | flops 138412032 | bytes 659712 | tf_op jit(solution)/shard_map/dot_general | solution.py:54
  34.6 4.1 %all-to-all-start.1 = ((f32[32,1,8,128]{3,2,1,0:T(8,128)}), f32[32,1,8,128]{3,2,1,0:T(8,128)S(1)}, u32[]{:S(2)}, u32[]{:S(2)}) async-start(f32[32,1,8,128]{3,2,1,0:T(8,128)} %convolution_bitcast_fusion), calls=%async_computation.1 | async-start | bytes 262144 | tf_op jit(solution)/shard_map/all_to_all | solution.py:57
  38.7 9.4 %all-to-all-done.1 = f32[32,1,8,128]{3,2,1,0:T(8,128)S(1)} async-done(((f32[32,1,8,128]{3,2,1,0:T(8,128)}), f32[32,1,8,128]{3,2,1,0:T(8,128)S(1)}, u32[]{:S(2)}, u32[]{:S(2)}) %all-to-all-start.1) | async-done | bytes 131104 | tf_op jit(solution)/shard_map/all_to_all | solution.py:57
  48.1 0.6 gather_fusion
  48.9 0.8 broadcast_in_dim.77
  49.7 6.5 %all-to-all-start.2 = ((f32[8,128,128]{2,1,0:T(8,128)}), f32[8,128,128]{2,1,0:T(8,128)S(1)}, u32[]{:S(2)}, u32[]{:S(2)}) async-start(f32[8,128,128]{2,1,0:T(8,128)} %broadcast_in_dim.77), calls=%async_computation.2 | async-start | bytes 1048576 | tf_op jit(solution)/shard_map/all_to_all | solution.py:9
  56.4 0.6 convert_reduce_fusion
  57.0 8.8 %all-to-all-done.2 = f32[8,128,128]{2,1,0:T(8,128)S(1)} async-done(((f32[8,128,128]{2,1,0:T(8,128)}), f32[8,128,128]{2,1,0:T(8,128)S(1)}, u32[]{:S(2)}, u32[]{:S(2)}) %all-to-all-start.2) | async-done | bytes 524320 | tf_op jit(solution)/shard_map/all_to_all | solution.py:9
  65.8 0.6 select_reduce_fusion
  66.4 0.7 pad_maximum_fusion
  67.0 0.6 broadcast_in_dim.82
  67.7 5.8 %all-to-all-start.3 = ((f32[32,1,129]{2,1,0:T(1,128)}), f32[32,1,129]{2,1,0:T(1,128)S(1)}, u32[]{:S(2)}, u32[]{:S(2)}) async-start(f32[32,1,129]{2,1,0:T(1,128)} %broadcast_in_dim.82), calls=%async_computation.3 | async-start | bytes 65536 | tf_op jit(solution)/shard_map/all_to_all | solution.py:9
  73.5 0.1 select_reduce_fusion.1
  73.6 8.2 %all-to-all-done.3 = f32[32,1,129]{2,1,0:T(1,128)S(1)} async-done(((f32[32,1,129]{2,1,0:T(1,128)}), f32[32,1,129]{2,1,0:T(1,128)S(1)}, u32[]{:S(2)}, u32[]{:S(2)}) %all-to-all-start.3) | async-done | bytes 16544 | tf_op jit(solution)/shard_map/all_to_all | solution.py:9
  81.8 0.5 slice.7
  82.3 0.6 slice_divide_fusion
  82.9 0.6 divide_subtract_fusion
  (28 shorter events, 1.0 us)
Async XLA Ops:
  0.6 32.2 %copy-start = (bf16[1,2048,128]{2,1,0:T(8,128)(2,1)S(1)}, bf16[1,2048,128]{2,1,0:T(8,128)(2,1)}, u32[]{:S(2)}) copy-start(bf16[1,2048,128]{2,1,0:T(8,128)(2,1)} %param.3) | copy-start | bytes 1572868
  13.5 18.9 %all-to-all-start = ((s32[32,1,8]{2,1,0:T(1,128)}), s32[32,1,8]{2,1,0:T(1,128)S(1)}, u32[]{:S(2)}, u32[]{:S(2)}) async-start(s32[32,1,8]{2,1,0:T(1,128)} %copy.26), calls=%async_computation | async-start | bytes 32768 | tf_op jit(solution)/shard_map/all_to_all | solution.py:45
  34.6 13.6 %all-to-all-start.1 = ((f32[32,1,8,128]{3,2,1,0:T(8,128)}), f32[32,1,8,128]{3,2,1,0:T(8,128)S(1)}, u32[]{:S(2)}, u32[]{:S(2)}) async-start(f32[32,1,8,128]{3,2,1,0:T(8,128)} %convolution_bitcast_fusion), calls=%async_computation.1 | async-start | bytes 262144 | tf_op jit(solution)/shard_map/all_to_all | solution.py:57
  49.7 6.5 %copy-start.1 = (s32[2]{0:T(128)S(1)}, s32[2]{0:T(128)}, u32[]{:S(2)}) copy-start(s32[2]{0:T(128)} %param.5) | copy-start | bytes 28
  49.7 16.0 %all-to-all-start.2 = ((f32[8,128,128]{2,1,0:T(8,128)}), f32[8,128,128]{2,1,0:T(8,128)S(1)}, u32[]{:S(2)}, u32[]{:S(2)}) async-start(f32[8,128,128]{2,1,0:T(8,128)} %broadcast_in_dim.77), calls=%async_computation.2 | async-start | bytes 1048576 | tf_op jit(solution)/shard_map/all_to_all | solution.py:9
  67.7 14.1 %all-to-all-start.3 = ((f32[32,1,129]{2,1,0:T(1,128)}), f32[32,1,129]{2,1,0:T(1,128)S(1)}, u32[]{:S(2)}, u32[]{:S(2)}) async-start(f32[32,1,129]{2,1,0:T(1,128)} %broadcast_in_dim.82), calls=%async_computation.3 | async-start | bytes 65536 | tf_op jit(solution)/shard_map/all_to_all | solution.py:9
where the time goes:
time: 84 us; the launch traced here: 83.6 us
  waiting for transfers between devices  34.1 us (41%)
  starting transfers between devices  27.4 us (33%)
  local copies, waits for them, and re-layouts  14.8 us (18%)
  other arithmetic  4.74 us (6%)
  matrix products  1.7 us (2%)
    all_to_all x2, waiting for transfers between devices, copy_for_each(): return lax.all_to_all(copies, axis, split_axis=0, concat_axis=0, tiled=True)  16.9 us
    all_to_all x2, starting transfers between devices, copy_for_each(): return lax.all_to_all(copies, axis, split_axis=0, concat_axis=0, tiled=True)  12.3 us
    scatter x2, local copies, waits for them, and re-layouts, routed_sums(): outgoing = jnp.full((n_lataxis, seg_count, slot_limit), -1, jnp.int32).at...  11.6 us
    all_to_all x1, starting transfers between devices, routed_sums(): lax.all_to_all(outgoing, 'lat', split_axis=0, concat_axis=0, tiled=True)  11 us
    all_to_all x1, waiting for transfers between devices, routed_sums(): lax.all_to_all(stacked, 'lat', split_axis=0, concat_axis=0, tiled=True)  9.4 us
    all_to_all x1, waiting for transfers between devices, routed_sums(): lax.all_to_all(outgoing, 'lat', split_axis=0, concat_axis=0, tiled=True)  7.79 us
    all_to_all x1, starting transfers between devices, routed_sums(): lax.all_to_all(stacked, 'lat', split_axis=0, concat_axis=0, tiled=True)  4.12 us
    dot_general x1, matrix products, routed_sums(): jnp.dot(weights.astype(jnp.bfloat16), coh_map[0], preferred_element_type=...  1.7 us
  transfers between devices with their start and end apart: 4, of which 4 were waited for; matrix products, arithmetic and copies ran while one was open for 1% of the time, Pallas kernels for 0%

commit v1 on v0

v1 whole, which is shorter than its diff:
```python
import functools

import jax
import jax.numpy as jnp
from jax import lax
from jax.experimental import pallas as pl
from jax.experimental.pallas import tpu as pltpu
from jax.sharding import PartitionSpec as P

MESH = pl.DeviceIdType.MESH
PER_BIN = 256
SUB = 4
PAIR = 2
LIVE = 4.0
VALID = 4096.0


def wait_bytes(ref, sem):
    pltpu.make_async_copy(ref, ref, sem).wait()


def kernel(
    n_seg,
    n_lat,
    map_ref,
    pos_ref,
    cnt_ref,
    stat_ref,
    exc_ref,
    table,
    note,
    heard,
    pair_note,
    rows_out,
    rows_in,
    pick,
    part,
    table_sem,
    note_send,
    heard_sem,
    pair_sem,
    rows_send,
    rows_sem,
    part_send,
    part_sem,
):
    n_y = n_seg // PAIR
    n_z = n_lat // SUB
    bins, width = table.shape
    points = pos_ref.shape[1]
    blocks = exc_ref.shape[0]
    block_size = points // blocks
    slots = 2 * points // n_lat
    span = bins * PER_BIN
    f32, bf16, i32 = jnp.float32, jnp.bfloat16, jnp.int32

    seg = lax.axis_index("seg")
    lat = lax.axis_index("lat")
    group, y = seg // n_y, seg % n_y
    other_seg = (PAIR - 1 - group) * n_y + y
    z, q = lat // SUB, lat % SUB

    def lat_at(t):
        g, s = t // SUB, t % SUB
        odd = g % 2
        dz = n_z // 2 + (1 - odd) * (g // 2) - odd * ((g + 1) // 2)
        return ((z + dz) % n_z) * SUB + (q + s + 1) % SUB

    load = pltpu.make_async_copy(map_ref.at[0], table, table_sem)
    load.start()

    barrier = pltpu.get_barrier_semaphore()

    def greet(t, _):
        d = lat_at(t)
        pl.semaphore_signal(barrier, inc=1, device_id=(seg, d), device_id_type=MESH)
        pl.semaphore_signal(barrier, inc=1, device_id=(other_seg, d), device_id_type=MESH)
        return _

    lax.fori_loop(0, n_lat - 1, greet, 0)
    pl.semaphore_signal(barrier, inc=1, device_id=(other_seg, lat), device_id_type=MESH)
    for k in range(1, n_y):
        peer = group * n_y + (y + k) % n_y
        pl.semaphore_signal(barrier, inc=1, device_id=(peer, lat), device_id_type=MESH)

    lane = lax.broadcasted_iota(i32, (1, points), 1)
    limit = jnp.zeros((1, points), i32)
    for b in range(blocks):
        limit = jnp.where(lane // block_size == b, cnt_ref[b] + b * block_size, limit)
    note[0:1, :] = pos_ref[...]
    note[1:2, :] = jnp.where(lane < limit, 1, 0)

    pl.semaphore_wait(barrier, 2 * n_lat - 1 + n_y - 1)

    def tell(t, _):
        pltpu.make_async_remote_copy(
            src_ref=note,
            dst_ref=heard.at[lat],
            send_sem=note_send,
            recv_sem=heard_sem,
            device_id=(seg, lat_at(t)),
            device_id_type=MESH,
        ).start()
        return _

    lax.fori_loop(0, n_lat - 1, tell, 0)
    pltpu.make_async_remote_copy(
        src_ref=note,
        dst_ref=pair_note,
        send_sem=note_send,
        recv_sem=pair_sem,
        device_id=(other_seg, lat),
        device_id_type=MESH,
    ).start()
    pltpu.make_async_copy(note, heard.at[lat], heard_sem).start()

    before_mat = jnp.where(
        lax.broadcasted_iota(i32, (points, points), 0)
        < lax.broadcasted_iota(i32, (points, points), 1),
        1.0,
        0.0,
    ).astype(bf16)

    load.wait()
    wait_bytes(heard, heard_sem)

    pos = heard[:, 0, :]
    ok = heard[:, 1, :]
    rel = pos - lat * span
    hit = (rel >= 0) & (rel < span)
    before = jnp.dot(
        jnp.where(hit, 1.0, 0.0).astype(bf16), before_mat, preferred_element_type=f32
    )
    key = jnp.where(hit, before, -1.0)
    coded = jnp.where(hit, rel.astype(f32) * (1.0 / PER_BIN) + LIVE + ok.astype(f32) * VALID, 0.0)
    slot_id = lax.broadcasted_iota(i32, (n_lat, slots, points), 1).astype(f32)
    chosen = jnp.where(key[:, None, :] == slot_id, coded[:, None, :], 0.0)
    code = jnp.sum(chosen, axis=2, keepdims=True).reshape(n_lat * slots, 1)
    is_valid = code >= VALID
    where_ = code - jnp.where(is_valid, VALID + LIVE, LIVE)
    bin_id = lax.broadcasted_iota(i32, (1, bins), 1).astype(f32)
    weights = jnp.maximum(1.0 - jnp.abs(where_ - bin_id), 0.0).astype(bf16)
    rows = jnp.dot(weights, table[...], preferred_element_type=f32)
    valid_sum = jnp.sum(jnp.where(is_valid, rows, 0.0), axis=0, keepdims=True)
    rows_out[:, 0:slots, :] = rows.reshape(n_lat, slots, width)
    rows_out[:, slots : slots + 1, :] = jnp.broadcast_to(valid_sum[None], (n_lat, 1, width))

    def give(t, _):
        d = lat_at(t)
        pltpu.make_async_remote_copy(
            src_ref=rows_out.at[d],
            dst_ref=rows_in.at[group, lat],
            send_sem=rows_send.at[1],
            recv_sem=rows_sem.at[group],
            device_id=(other_seg, d),
            device_id_type=MESH,
        ).start()
        pltpu.make_async_remote_copy(
            src_ref=rows_out.at[d],
            dst_ref=rows_in.at[group, lat],
            send_sem=rows_send.at[0],
            recv_sem=rows_sem.at[group],
            device_id=(seg, d),
            device_id_type=MESH,
        ).start()
        return _

    lax.fori_loop(0, n_lat - 1, give, 0)
    pltpu.make_async_remote_copy(
        src_ref=rows_out.at[lat],
        dst_ref=rows_in.at[group, lat],
        send_sem=rows_send.at[1],
        recv_sem=rows_sem.at[group],
        device_id=(other_seg, lat),
        device_id_type=MESH,
    ).start()
    pltpu.make_async_copy(rows_out.at[lat], rows_in.at[group, lat], rows_sem.at[group]).start()

    wait_bytes(pair_note, pair_sem)
    dest_id = lax.broadcasted_iota(i32, (n_lat, points), 0)
    flat_id = lax.broadcasted_iota(i32, (n_lat * slots, points), 0).astype(f32)
    for g in range(PAIR):
        mine = jnp.where(group == g, note[0:1, :], pair_note[0:1, :])
        dest = mine // span
        at_dest = jnp.where(dest == dest_id, 1.0, 0.0)
        ahead = jnp.dot(at_dest.astype(bf16), before_mat, preferred_element_type=f32)
        slot = jnp.sum(at_dest * ahead, axis=0, keepdims=True)
        flat = dest.astype(f32) * slots + slot
        choice = jnp.where(flat_id == flat, 1.0, 0.0)
        pick[:, g * n_lat * slots : (g + 1) * n_lat * slots] = choice.T.astype(bf16)
    total_count = jnp.sum(ok.astype(f32))

    for g in range(PAIR):
        wait_bytes(rows_in.at[g], rows_sem.at[g])
    got = rows_in[:, :, 0:slots, :].reshape(PAIR * n_lat * slots, width)
    high = got.astype(bf16)
    rest = got - high.astype(f32)
    mid = rest.astype(bf16)
    low = (rest - mid.astype(f32)).astype(bf16)
    chooser = pick[...]
    own = (
        jnp.dot(chooser, low, preferred_element_type=f32)
        + jnp.dot(chooser, mid, preferred_element_type=f32)
        + jnp.dot(chooser, high, preferred_element_type=f32)
    )
    part[y, 0:points, :] = own
    sums = rows_in[:, :, slots, :].reshape(PAIR * n_lat, width)
    part[y, points : points + 8, :] = jnp.broadcast_to(
        jnp.sum(sums, axis=0, keepdims=True), (8, width)
    )

    for k in range(1, n_y):
        peer = group * n_y + (y + k % (n_y - 1) + 1) % n_y
        pltpu.make_async_remote_copy(
            src_ref=part.at[y],
            dst_ref=part.at[y],
            send_sem=part_send,
            recv_sem=part_sem,
            device_id=(peer, lat),
            device_id_type=MESH,
        ).start()
    wait_bytes(part.at[0 : n_y - 1], part_sem)

    all_sum = part[0]
    for k in range(1, n_y):
        all_sum = all_sum + part[k]
    stat = all_sum[0:points] * (1.0 / n_seg)
    stat_ref[...] = stat.astype(bf16)
    global_mean = all_sum[points : points + 1] * (1.0 / n_seg) / total_count
    row_id = lax.broadcasted_iota(i32, (block_size, width), 0)
    for b in range(blocks):
        count = cnt_ref[b]
        block = stat[b * block_size : (b + 1) * block_size]
        block_sum = jnp.sum(jnp.where(row_id < count, block, 0.0), axis=0, keepdims=True)
        exc_ref[b : b + 1, :] = block_sum / count.astype(f32) - global_mean

    wait_bytes(heard, note_send)
    wait_bytes(rows_in.at[0, 0 : n_lat - 1], rows_send.at[0])
    wait_bytes(rows_in.at[0], rows_send.at[1])
    wait_bytes(part.at[0 : n_y - 1], part_send)


def shards(coh_map, positions, counts):
    n_seg, n_lat = lax.axis_size("seg"), lax.axis_size("lat")
    _, bins, width = coh_map.shape
    points = positions.shape[1]
    blocks = counts.shape[0]
    slots = 2 * points // n_lat
    n_y = n_seg // PAIR
    dma = pltpu.SemaphoreType.DMA
    vmem = pl.BlockSpec(memory_space=pltpu.VMEM)
    return pl.pallas_call(
        functools.partial(kernel, n_seg, n_lat),
        out_shape=(
            jax.ShapeDtypeStruct((points, width), jnp.bfloat16),
            jax.ShapeDtypeStruct((blocks, width), jnp.float32),
        ),
        in_specs=[
            pl.BlockSpec(memory_space=pl.ANY),
            vmem,
            pl.BlockSpec(memory_space=pltpu.SMEM),
        ],
        out_specs=(vmem, vmem),
        scratch_shapes=[
            pltpu.VMEM((bins, width), jnp.bfloat16),
            pltpu.VMEM((2, points), jnp.int32),
            pltpu.VMEM((n_lat, 2, points), jnp.int32),
            pltpu.VMEM((2, points), jnp.int32),
            pltpu.VMEM((n_lat, slots + 1, width), jnp.float32),
            pltpu.VMEM((PAIR, n_lat, slots + 1, width), jnp.float32),
            pltpu.VMEM((points, PAIR * n_lat * slots), jnp.bfloat16),
            pltpu.VMEM((n_y, points + 8, width), jnp.float32),
            dma,
            dma,
            dma,
            dma,
            dma((2,)),
            dma((PAIR,)),
            dma,
            dma,
        ],
        compiler_params=pltpu.CompilerParams(collective_id=0, has_side_effects=True),
    )(coh_map, positions, counts)


def solution(mesh):
    in_specs = (P("seg", "lat", None), P("seg", "lat"), P("lat"))
    out_specs = (P("lat", None), P("lat", None))
    return jax.shard_map(shards, mesh=mesh, in_specs=in_specs, out_specs=out_specs, check_vma=False)
```

time: 84 us -> 37.8 us (0.45)
  Pallas kernels: 0 us -> 35.1 us
  waiting for transfers between devices: 34.1 us -> 0 us
  starting transfers between devices: 27.4 us -> 0 us
  local copies, waits for them, and re-layouts: 14.8 us -> 1.94 us
  other arithmetic: 4.74 us -> 0 us
  matrix products: 1.7 us -> 0 us
    pallas_call x0 -> x1, Pallas kernels: none -> 35.1 us  [shards(): pl.pallas_call(functools.partial(kernel, n_seg, n_lat), out_shape=(jax.Sh...]
    all_to_all x4 -> x0, waiting for transfers between devices: 34.1 us -> none  [the longest x2 16.9 us: copy_for_each(): return lax.all_to_all(copies, axis, split_axis=0, concat_axis=0, tiled=True)]
    all_to_all x4 -> x0, starting transfers between devices: 27.4 us -> none  [the longest x2 12.3 us: copy_for_each(): return lax.all_to_all(copies, axis, split_axis=0, concat_axis=0, tiled=True)]
    scatter x2 -> x0, local copies, waits for them, and re-layouts: 11.6 us -> none  [routed_sums(): outgoing = jnp.full((n_lataxis, seg_count, slot_limit), -1, jnp.int32).at...]
    unnamed x4, local copies, waits for them, and re-layouts: 0.01 us -> 1.94 us
    dot_general x1 -> x0, matrix products: 1.7 us -> none  [routed_sums(): jnp.dot(weights.astype(jnp.bfloat16), coh_map[0], preferred_element_type=...]
    reduce_sum x6 -> x0, other arithmetic: 1.58 us -> none  [the longest x1 0.63 us: shards(): jnp.sum(block_sums, axis=0)]
    broadcast_in_dim x3 -> x0, local copies, waits for them, and re-layouts: 1.44 us -> none  [the longest x2 1.44 us: copy_for_each(): copies = jnp.broadcast_to(shard, (lax.axis_size(axis), *shard.shape))]
  transfers between devices with their start and end apart: 4 -> 0, of which waited for: 4 -> 0; matrix products, arithmetic and copies ran while one was open for 1% -> 0% of each run, Pallas kernels for 0% -> 0%
where the time goes in v1:
time: 37.8 us; the launch traced here: 37.7 us
  Pallas kernels  35.1 us (93%)
  local copies, waits for them, and re-layouts  1.94 us (5%)
  between operations  0.65 us (2%)
    pallas_call x1, Pallas kernels, shards(): pl.pallas_call(functools.partial(kernel, n_seg, n_lat), out_shape=(jax.Sh...  35.1 us
    unnamed x4, local copies, waits for them, and re-layouts  1.94 us

profile of v1, /device:TPU:1, one launch (start us, length us, event | category | flops | bytes accessed | tf_op | source)
XLA Modules:
  0.0 37.7 jit_solution(6481128970258805003)
XLA Ops:
  0.6 35.1 %shard_map.50 = (bf16[128,128]{1,0:T(8,128)(2,1)}, f32[2,128]{1,0:T(2,128)}) custom-call(bf16[1,2048,128]{2,1,0:T(8,128)(2,1)} %map_ref.1, s32[1,128]{1,0:T(1,128)} %pos_ref.1, s32[2]{0:T(128)} %cnt_ref.1), custom_call_target="tpu_custom_call" | custom-call | tf_op jit(solution)/shard_map/pallas_call | solution.py:252
  35.7 0.0 copy-start
  35.7 1.4 %copy.7 = bf16[128,128]{1,0:T(8,128)(2,1)} copy(bf16[128,128]{1,0:T(8,128)(2,1)} %get-tuple-element.4) | data formatting | bytes 65536
  37.1 0.0 copy-done
  37.1 0.6 %copy.8 = f32[2,128]{1,0:T(2,128)} copy(f32[2,128]{1,0:T(2,128)S(1)} %copy-done) | data formatting | bytes 2048
Async XLA Ops:
  35.7 1.4 %copy-start = (f32[2,128]{1,0:T(2,128)S(1)}, f32[2,128]{1,0:T(2,128)}, u32[]{:S(2)}) copy-start(f32[2,128]{1,0:T(2,128)} %get-tuple-element.5) | copy-start | bytes 3076

commit v2 on v1

v2 whole, which is shorter than its diff:
```python
import functools

import jax
import jax.numpy as jnp
from jax import lax
from jax.experimental import pallas as pl
from jax.experimental.pallas import tpu as pltpu
from jax.sharding import PartitionSpec as P

MESH = pl.DeviceIdType.MESH
PER_BIN = 256
SUB = 4
PAIR = 2
LIVE = 4.0
VALID = 4096.0


def wait_bytes(ref, sem):
    pltpu.make_async_copy(ref, ref, sem).wait()


def kernel(
    n_seg,
    n_lat,
    map_ref,
    pos_ref,
    cnt_ref,
    stat_ref,
    exc_ref,
    table,
    note,
    heard,
    pair_note,
    rows_out,
    rows_in,
    sum_out,
    sum_in,
    pick,
    part,
    table_sem,
    note_send,
    heard_sem,
    pair_sem,
    rows_send,
    rows_sem,
    sum_send,
    sum_sem,
    part_send,
    part_sem,
):
    n_y = n_seg // PAIR
    n_z = n_lat // SUB
    half = n_z // 2
    bins, width = table.shape
    points = pos_ref.shape[1]
    blocks = exc_ref.shape[0]
    block_size = points // blocks
    slots = 2 * points // n_lat
    span = bins * PER_BIN
    f32, bf16, i32 = jnp.float32, jnp.bfloat16, jnp.int32

    seg = lax.axis_index("seg")
    lat = lax.axis_index("lat")
    group, y = lax.div(seg, n_y), lax.rem(seg, n_y)
    other = PAIR - 1 - group
    other_seg = other * n_y + y
    z, q = lax.div(lat, SUB), lax.rem(lat, SUB)

    offsets = [0] + [o for k in range(1, half) for o in (k, n_z - k)] + [half]
    waves = [(0, 1)] + [(2 * k - 1, 2 * k + 1) for k in range(1, half)] + [(n_z - 1, n_z)]
    first_at = [lax.rem(z + o, n_z) * SUB for o in offsets]
    near_q = [lax.rem(q + s, SUB) for s in range(1, SUB)]

    def peers(i):
        if i == 0:
            return [(nq, first_at[0] + nq) for nq in near_q]
        return [(s, first_at[i] + s) for s in range(SUB)]

    y_peers = [group * n_y + lax.rem(y + k, n_y) for k in range(1, n_y)]
    far_first = list(range(n_z - 1, -1, -1))

    load = pltpu.make_async_copy(map_ref.at[0], table, table_sem)
    load.start()

    barrier = pltpu.get_barrier_semaphore()
    for i in far_first:
        for _, d in peers(i):
            pl.semaphore_signal(barrier, inc=1, device_id=(seg, d), device_id_type=MESH)
    pl.semaphore_signal(barrier, inc=1, device_id=(other_seg, lat), device_id_type=MESH)
    for peer in y_peers:
        pl.semaphore_signal(barrier, inc=1, device_id=(peer, lat), device_id_type=MESH)

    lane = lax.broadcasted_iota(i32, (1, points), 1)
    limit = jnp.zeros((1, points), i32)
    for b in range(blocks):
        limit = jnp.where(lane // block_size == b, cnt_ref[b] + b * block_size, limit)
    note[0:1, :] = pos_ref[...]
    note[1:2, :] = jnp.where(lane < limit, 1, 0)

    before_mat = jnp.where(
        lax.broadcasted_iota(i32, (points, points), 0)
        < lax.broadcasted_iota(i32, (points, points), 1),
        1.0,
        0.0,
    ).astype(bf16)
    dest_id = lax.broadcasted_iota(i32, (n_lat, points), 0)
    flat_id = lax.broadcasted_iota(i32, (n_lat * slots, points), 0).astype(f32)

    def chooser(positions):
        dest = lax.div(positions, span)
        at_dest = jnp.where(dest == dest_id, 1.0, 0.0)
        ahead = jnp.dot(at_dest.astype(bf16), before_mat, preferred_element_type=f32)
        slot = jnp.sum(at_dest * ahead, axis=0, keepdims=True)
        flat = dest.astype(f32) * slots + slot
        return jnp.where(flat_id == flat, 1.0, 0.0).T.astype(bf16)

    pick[group] = chooser(pos_ref[...])

    pl.semaphore_wait(barrier, n_lat - 1 + 1 + n_y - 1)

    for i in far_first:
        w = min(offsets[i], n_z - offsets[i])
        back = offsets.index((n_z - offsets[i]) % n_z)
        for _, d in peers(i):
            pltpu.make_async_remote_copy(
                src_ref=note,
                dst_ref=heard.at[back, q],
                send_sem=note_send,
                recv_sem=heard_sem.at[w],
                device_id=(seg, d),
                device_id_type=MESH,
            ).start()
        if i == n_z - 1:
            pltpu.make_async_remote_copy(
                src_ref=note,
                dst_ref=pair_note,
                send_sem=note_send,
                recv_sem=pair_sem,
                device_id=(other_seg, lat),
                device_id_type=MESH,
            ).start()
    pltpu.make_async_copy(note, heard.at[0, q], heard_sem.at[0]).start()

    load.wait()
    bin_id = lax.broadcasted_iota(i32, (1, bins), 1).astype(f32)
    total_sum = jnp.zeros((1, width), f32)
    total_count = jnp.zeros((1, 1), f32)
    for k, (lo, hi) in enumerate(waves):
        wait_bytes(heard.at[lo:hi], heard_sem.at[k])
        n = (hi - lo) * SUB
        pos = heard[lo:hi, :, 0, :].reshape(n, points)
        ok = heard[lo:hi, :, 1, :].reshape(n, points)
        rel = pos - lat * span
        hit = (rel >= 0) & (rel < span)
        before = jnp.dot(
            jnp.where(hit, 1.0, 0.0).astype(bf16), before_mat, preferred_element_type=f32
        )
        key = jnp.where(hit, before, -1.0)
        valid = ok.astype(f32)
        coded = jnp.where(hit, rel.astype(f32) * (1.0 / PER_BIN) + LIVE + valid * VALID, 0.0)
        slot_id = lax.broadcasted_iota(i32, (n, slots, points), 1).astype(f32)
        chosen = jnp.where(key[:, None, :] == slot_id, coded[:, None, :], 0.0)
        code = jnp.sum(chosen, axis=2, keepdims=True).reshape(n * slots, 1)
        is_valid = code >= VALID
        at_bin = code - jnp.where(is_valid, VALID + LIVE, LIVE)
        weights = jnp.maximum(1.0 - jnp.abs(at_bin - bin_id), 0.0).astype(bf16)
        rows = jnp.dot(weights, table[...], preferred_element_type=f32)
        rows_out[lo:hi] = rows.reshape(hi - lo, SUB, slots, width)
        if k == 0:
            wait_bytes(pair_note, pair_sem)

        for i in range(lo, hi):
            targets = [(other_seg, s, first_at[i] + s, 1) for s in range(SUB)]
            targets += [(seg, s, d, 0) for s, d in peers(i)]
            for g, s, d, which in targets:
                pltpu.make_async_remote_copy(
                    src_ref=rows_out.at[i, s],
                    dst_ref=rows_in.at[group, lat],
                    send_sem=rows_send.at[which],
                    recv_sem=rows_sem.at[group],
                    device_id=(g, d),
                    device_id_type=MESH,
                ).start()
            if i == 0:
                pltpu.make_async_copy(
                    rows_out.at[0, q], rows_in.at[group, lat], rows_sem.at[group]
                ).start()
        total_sum += jnp.sum(jnp.where(is_valid, rows, 0.0), axis=0, keepdims=True)
        total_count += jnp.sum(valid, keepdims=True)

    sum_out[...] = jnp.broadcast_to(total_sum, (8, width))
    for i in far_first:
        targets = [(other_seg, s, first_at[i] + s, 1) for s in range(SUB)]
        targets += [(seg, s, d, 0) for s, d in peers(i)]
        for g, s, d, which in targets:
            pltpu.make_async_remote_copy(
                src_ref=sum_out.at[0:1],
                dst_ref=sum_in.at[group, lat],
                send_sem=sum_send.at[which],
                recv_sem=sum_sem,
                device_id=(g, d),
                device_id_type=MESH,
            ).start()
    pltpu.make_async_copy(sum_out.at[0:1], sum_in.at[group, lat], sum_sem).start()

    pick[other] = chooser(pair_note[0:1, :])

    own = jnp.zeros((points, width), f32)
    for g in range(PAIR):
        wait_bytes(rows_in.at[g], rows_sem.at[g])
        got = rows_in[g].reshape(n_lat * slots, width)
        high = got.astype(bf16)
        rest = got - high.astype(f32)
        mid = rest.astype(bf16)
        low = (rest - mid.astype(f32)).astype(bf16)
        choice = pick[g]
        own += (
            jnp.dot(choice, low, preferred_element_type=f32)
            + jnp.dot(choice, mid, preferred_element_type=f32)
            + jnp.dot(choice, high, preferred_element_type=f32)
        )
    part[y, 0:points, :] = own
    wait_bytes(sum_in, sum_sem)
    sums = sum_in[...].reshape(PAIR * n_lat, width)
    part[y, points : points + 8, :] = jnp.broadcast_to(
        jnp.sum(sums, axis=0, keepdims=True), (8, width)
    )

    for peer in y_peers[1:] + y_peers[:1]:
        pltpu.make_async_remote_copy(
            src_ref=part.at[y],
            dst_ref=part.at[y],
            send_sem=part_send,
            recv_sem=part_sem,
            device_id=(peer, lat),
            device_id_type=MESH,
        ).start()
    wait_bytes(part.at[0 : n_y - 1], part_sem)

    all_sum = part[0]
    for k in range(1, n_y):
        all_sum = all_sum + part[k]
    stat = all_sum[0:points] * (1.0 / n_seg)
    stat_ref[...] = stat.astype(bf16)
    global_mean = all_sum[points : points + 1] * (1.0 / n_seg) / total_count
    row_id = lax.broadcasted_iota(i32, (block_size, width), 0)
    for b in range(blocks):
        count = cnt_ref[b]
        block = stat[b * block_size : (b + 1) * block_size]
        block_sum = jnp.sum(jnp.where(row_id < count, block, 0.0), axis=0, keepdims=True)
        exc_ref[b : b + 1, :] = block_sum / count.astype(f32) - global_mean

    wait_bytes(heard, note_send)
    wait_bytes(rows_in.at[0, 0 : n_lat - 1], rows_send.at[0])
    wait_bytes(rows_in.at[0], rows_send.at[1])
    wait_bytes(sum_in.at[0, 0 : n_lat - 1], sum_send.at[0])
    wait_bytes(sum_in.at[0], sum_send.at[1])
    wait_bytes(part.at[0 : n_y - 1], part_send)


def shards(coh_map, positions, counts):
    n_seg, n_lat = lax.axis_size("seg"), lax.axis_size("lat")
    _, bins, width = coh_map.shape
    points = positions.shape[1]
    blocks = counts.shape[0]
    slots = 2 * points // n_lat
    n_y, n_z = n_seg // PAIR, n_lat // SUB
    dma = pltpu.SemaphoreType.DMA
    vmem = pl.BlockSpec(memory_space=pltpu.VMEM)
    return pl.pallas_call(
        functools.partial(kernel, n_seg, n_lat),
        out_shape=(
            jax.ShapeDtypeStruct((points, width), jnp.bfloat16),
            jax.ShapeDtypeStruct((blocks, width), jnp.float32),
        ),
        in_specs=[
            pl.BlockSpec(memory_space=pl.ANY),
            vmem,
            pl.BlockSpec(memory_space=pltpu.SMEM),
        ],
        out_specs=(vmem, vmem),
        scratch_shapes=[
            pltpu.VMEM((bins, width), jnp.bfloat16),
            pltpu.VMEM((2, points), jnp.int32),
            pltpu.VMEM((n_z, SUB, 2, points), jnp.int32),
            pltpu.VMEM((2, points), jnp.int32),
            pltpu.VMEM((n_z, SUB, slots, width), jnp.float32),
            pltpu.VMEM((PAIR, n_lat, slots, width), jnp.float32),
            pltpu.VMEM((8, width), jnp.float32),
            pltpu.VMEM((PAIR, n_lat, 1, width), jnp.float32),
            pltpu.VMEM((PAIR, points, n_lat * slots), jnp.bfloat16),
            pltpu.VMEM((n_y, points + 8, width), jnp.float32),
            dma,
            dma,
            dma((n_z // 2 + 1,)),
            dma,
            dma((2,)),
            dma((PAIR,)),
            dma((2,)),
            dma,
            dma,
            dma,
        ],
        compiler_params=pltpu.CompilerParams(collective_id=0, has_side_effects=True),
    )(coh_map, positions, counts)


def solution(mesh):
    in_specs = (P("seg", "lat", None), P("seg", "lat"), P("lat"))
    out_specs = (P("lat", None), P("lat", None))
    return jax.shard_map(shards, mesh=mesh, in_specs=in_specs, out_specs=out_specs, check_vma=False)
```

time: 37.8 us -> 35.5 us (0.939)
  Pallas kernels: 35.1 us -> 32.8 us
    pallas_call x1, Pallas kernels: 35.1 us -> 32.8 us  [shards(): pl.pallas_call(functools.partial(kernel, n_seg, n_lat), out_shape=(jax.Sh...]
where the time goes in v2:
time: 35.5 us; the launch traced here: 35.4 us
  Pallas kernels  32.8 us (92%)
  local copies, waits for them, and re-layouts  1.94 us (5%)
  between operations  0.65 us (2%)
    pallas_call x1, Pallas kernels, shards(): pl.pallas_call(functools.partial(kernel, n_seg, n_lat), out_shape=(jax.Sh...  32.8 us
    unnamed x4, local copies, waits for them, and re-layouts  1.94 us

profile of v2, /device:TPU:1, one launch (start us, length us, event | category | flops | bytes accessed | tf_op | source)
XLA Modules:
  0.0 35.4 jit_solution(9582463435179747514)
XLA Ops:
  0.6 32.8 %shard_map.50 = (bf16[128,128]{1,0:T(8,128)(2,1)}, f32[2,128]{1,0:T(2,128)}) custom-call(bf16[1,2048,128]{2,1,0:T(8,128)(2,1)} %map_ref.1, s32[1,128]{1,0:T(1,128)} %pos_ref.1, s32[2]{0:T(128)} %cnt_ref.1), custom_call_target="tpu_custom_call" | custom-call | tf_op jit(solution)/shard_map/pallas_call | solution.py:270
  33.4 0.0 copy-start
  33.4 1.4 %copy.7 = bf16[128,128]{1,0:T(8,128)(2,1)} copy(bf16[128,128]{1,0:T(8,128)(2,1)} %get-tuple-element.4) | data formatting | bytes 65536
  34.8 0.0 copy-done
  34.8 0.6 %copy.8 = f32[2,128]{1,0:T(2,128)} copy(f32[2,128]{1,0:T(2,128)S(1)} %copy-done) | data formatting | bytes 2048
Async XLA Ops:
  33.4 1.4 %copy-start = (f32[2,128]{1,0:T(2,128)S(1)}, f32[2,128]{1,0:T(2,128)}, u32[]{:S(2)}) copy-start(f32[2,128]{1,0:T(2,128)} %get-tuple-element.5) | copy-start | bytes 3076

commit v3 on v2

--- a/solution.py
+++ b/solution.py
@@ -23,20 +23,24 @@
     n_seg,
     n_lat,
     map_ref,
-    pos_ref,
-    cnt_ref,
+    pos_hbm,
+    cnt_hbm,
     stat_ref,
     exc_ref,
     table,
+    cnt_ref,
     note,
     heard,
     pair_note,
     rows_out,
     rows_in,
     sum_out,
-    sum_in,
+    near_in,
+    far_in,
     pick,
     part,
+    pos_sem,
+    cnt_sem,
     table_sem,
     note_send,
     heard_sem,
@@ -44,7 +48,8 @@
     rows_send,
     rows_sem,
     sum_send,
-    sum_sem,
+    near_sem,
+    far_sem,
     part_send,
     part_sem,
 ):
@@ -52,7 +57,7 @@
     n_z = n_lat // SUB
     half = n_z // 2
     bins, width = table.shape
-    points = pos_ref.shape[1]
+    points = pos_hbm.shape[1]
     blocks = exc_ref.shape[0]
     block_size = points // blocks
     slots = 2 * points // n_lat
@@ -79,8 +84,11 @@
     y_peers = [group * n_y + lax.rem(y + k, n_y) for k in range(1, n_y)]
     far_first = list(range(n_z - 1, -1, -1))
 
+    load_pos = pltpu.make_async_copy(pos_hbm, note.at[0:1], pos_sem)
+    load_cnt = pltpu.make_async_copy(cnt_hbm, cnt_ref, cnt_sem)
     load = pltpu.make_async_copy(map_ref.at[0], table, table_sem)
-    load.start()
+    load_pos.start()
+    load_cnt.start()
 
     barrier = pltpu.get_barrier_semaphore()
     for i in far_first:
@@ -90,11 +98,13 @@
     for peer in y_peers:
         pl.semaphore_signal(barrier, inc=1, device_id=(peer, lat), device_id_type=MESH)
 
+    load.start()
+
     lane = lax.broadcasted_iota(i32, (1, points), 1)
     limit = jnp.zeros((1, points), i32)
+    load_cnt.wait()
     for b in range(blocks):
         limit = jnp.where(lane // block_size == b, cnt_ref[b] + b * block_size, limit)
-    note[0:1, :] = pos_ref[...]
     note[1:2, :] = jnp.where(lane < limit, 1, 0)
 
     before_mat = jnp.where(
@@ -114,7 +124,8 @@
         flat = dest.astype(f32) * slots + slot
         return jnp.where(flat_id == flat, 1.0, 0.0).T.astype(bf16)
 
-    pick[group] = chooser(pos_ref[...])
+    load_pos.wait()
+    pick[group] = chooser(note[0:1, :])
 
     pl.semaphore_wait(barrier, n_lat - 1 + 1 + n_y - 1)
 
@@ -188,22 +199,35 @@
         total_sum += jnp.sum(jnp.where(is_valid, rows, 0.0), axis=0, keepdims=True)
         total_count += jnp.sum(valid, keepdims=True)
 
-    sum_out[...] = jnp.broadcast_to(total_sum, (8, width))
-    for i in far_first:
-        targets = [(other_seg, s, first_at[i] + s, 1) for s in range(SUB)]
-        targets += [(seg, s, d, 0) for s, d in peers(i)]
-        for g, s, d, which in targets:
-            pltpu.make_async_remote_copy(
-                src_ref=sum_out.at[0:1],
-                dst_ref=sum_in.at[group, lat],
-                send_sem=sum_send.at[which],
-                recv_sem=sum_sem,
-                device_id=(g, d),
-                device_id_type=MESH,
-            ).start()
-    pltpu.make_async_copy(sum_out.at[0:1], sum_in.at[group, lat], sum_sem).start()
+    sum_out[0] = total_sum
+    near_in[group * SUB + q] = total_sum
+    for g, d in [(other_seg, first_at[0] + s) for s in range(SUB)] + [
+        (seg, d) for _, d in peers(0)
+    ]:
+        pltpu.make_async_remote_copy(
+            src_ref=sum_out.at[0],
+            dst_ref=near_in.at[group * SUB + q],
+            send_sem=sum_send.at[0],
+            recv_sem=near_sem,
+            device_id=(g, d),
+            device_id_type=MESH,
+        ).start()
 
     pick[other] = chooser(pair_note[0:1, :])
+
+    wait_bytes(near_in.at[0 : PAIR * SUB - 1], near_sem)
+    near_sum = jnp.sum(near_in[...], axis=0)
+    sum_out[1] = near_sum
+    far_in[z] = near_sum
+    for i in far_first[:-1]:
+        pltpu.make_async_remote_copy(
+            src_ref=sum_out.at[1],
+            dst_ref=far_in.at[z],
+            send_sem=sum_send.at[1],
+            recv_sem=far_sem,
+            device_id=(seg, first_at[i] + q),
+            device_id_type=MESH,
+        ).start()
 
     own = jnp.zeros((points, width), f32)
     for g in range(PAIR):
@@ -220,11 +244,8 @@
             + jnp.dot(choice, high, preferred_element_type=f32)
         )
     part[y, 0:points, :] = own
-    wait_bytes(sum_in, sum_sem)
-    sums = sum_in[...].reshape(PAIR * n_lat, width)
-    part[y, points : points + 8, :] = jnp.broadcast_to(
-        jnp.sum(sums, axis=0, keepdims=True), (8, width)
-    )
+    wait_bytes(far_in.at[0 : n_z - 1], far_sem)
+    part[y, points : points + 8, :] = jnp.broadcast_to(jnp.sum(far_in[...], axis=0), (8, width))
 
     for peer in y_peers[1:] + y_peers[:1]:
         pltpu.make_async_remote_copy(
@@ -253,9 +274,18 @@
     wait_bytes(heard, note_send)
     wait_bytes(rows_in.at[0, 0 : n_lat - 1], rows_send.at[0])
     wait_bytes(rows_in.at[0], rows_send.at[1])
-    wait_bytes(sum_in.at[0, 0 : n_lat - 1], sum_send.at[0])
-    wait_bytes(sum_in.at[0], sum_send.at[1])
+    wait_bytes(near_in.at[0 : PAIR * SUB - 1], sum_send.at[0])
+    wait_bytes(far_in.at[0 : n_z - 1], sum_send.at[1])
     wait_bytes(part.at[0 : n_y - 1], part_send)
+
+
+def put_out(stat_ref, exc_ref, stat_out, exc_out, stat_sem, exc_sem):
+    stat = pltpu.make_async_copy(stat_ref, stat_out, stat_sem)
+    exc = pltpu.make_async_copy(exc_ref, exc_out, exc_sem)
+    stat.start()
+    exc.start()
+    stat.wait()
+    exc.wait()
 
 
 def shards(coh_map, positions, counts):
@@ -267,29 +297,34 @@
     n_y, n_z = n_seg // PAIR, n_lat // SUB
     dma = pltpu.SemaphoreType.DMA
     vmem = pl.BlockSpec(memory_space=pltpu.VMEM)
-    return pl.pallas_call(
+    anywhere = pl.BlockSpec(memory_space=pl.ANY)
+    stat, excess = pl.pallas_call(
         functools.partial(kernel, n_seg, n_lat),
         out_shape=(
-            jax.ShapeDtypeStruct((points, width), jnp.bfloat16),
-            jax.ShapeDtypeStruct((blocks, width), jnp.float32),
+            pltpu.VMEM((points, width), jnp.bfloat16),
+            pltpu.VMEM((blocks, width), jnp.float32),
         ),
         in_specs=[
-            pl.BlockSpec(memory_space=pl.ANY),
-            vmem,
-            pl.BlockSpec(memory_space=pltpu.SMEM),
+            anywhere,
+            anywhere,
+            anywhere,
         ],
         out_specs=(vmem, vmem),
         scratch_shapes=[
             pltpu.VMEM((bins, width), jnp.bfloat16),
+            pltpu.SMEM((blocks,), jnp.int32),
             pltpu.VMEM((2, points), jnp.int32),
             pltpu.VMEM((n_z, SUB, 2, points), jnp.int32),
             pltpu.VMEM((2, points), jnp.int32),
             pltpu.VMEM((n_z, SUB, slots, width), jnp.float32),
             pltpu.VMEM((PAIR, n_lat, slots, width), jnp.float32),
-            pltpu.VMEM((8, width), jnp.float32),
-            pltpu.VMEM((PAIR, n_lat, 1, width), jnp.float32),
+            pltpu.VMEM((2, 1, width), jnp.float32),
+            pltpu.VMEM((PAIR * SUB, 1, width), jnp.float32),
+            pltpu.VMEM((n_z, 1, width), jnp.float32),
             pltpu.VMEM((PAIR, points, n_lat * slots), jnp.bfloat16),
             pltpu.VMEM((n_y, points + 8, width), jnp.float32),
+            dma,
+            dma,
             dma,
             dma,
             dma((n_z // 2 + 1,)),
@@ -300,9 +335,21 @@
             dma,
             dma,
             dma,
+            dma,
         ],
         compiler_params=pltpu.CompilerParams(collective_id=0, has_side_effects=True),
     )(coh_map, positions, counts)
+    in_vmem = functools.partial(pltpu.with_memory_space_constraint, memory_space=pltpu.VMEM)
+    return pl.pallas_call(
+        put_out,
+        out_shape=(
+            jax.ShapeDtypeStruct((points, width), jnp.bfloat16),
+            jax.ShapeDtypeStruct((blocks, width), jnp.float32),
+        ),
+        in_specs=[vmem, vmem],
+        out_specs=(anywhere, anywhere),
+        scratch_shapes=[dma, dma],
+    )(in_vmem(stat), in_vmem(excess))
 
 
 def solution(mesh):

time: 35.5 us -> 32.6 us (0.918)
  local copies, waits for them, and re-layouts: 1.94 us -> 0 us
  Pallas kernels: 32.8 us -> 31.8 us
    unnamed x4 -> x0, local copies, waits for them, and re-layouts: 1.94 us -> none
    pallas_call x1 -> x2, Pallas kernels: 32.8 us -> 31.8 us  [the longest x1 31.2 us: shards(): pl.pallas_call(functools.partial(kernel, n_seg, n_lat), out_shape=(pltpu....]
where the time goes in v3:
time: 32.6 us; the launch traced here: 32.5 us
  Pallas kernels  31.8 us (98%)
  between operations  0.64 us (2%)
    pallas_call x1, Pallas kernels, shards(): pl.pallas_call(functools.partial(kernel, n_seg, n_lat), out_shape=(pltpu....  31.2 us

profile of v3, /device:TPU:1, one launch (start us, length us, event | category | flops | bytes accessed | tf_op | source)
XLA Modules:
  0.0 32.5 jit_solution(9173266202794194881)
XLA Ops:
  0.6 31.2 %shard_map.50 = (bf16[128,128]{1,0:T(8,128)(2,1)S(1)}, f32[2,128]{1,0:T(2,128)S(1)}) custom-call(bf16[1,2048,128]{2,1,0:T(8,128)(2,1)} %map_ref.1, s32[1,128]{1,0:T(1,128)} %pos_hbm.1, s32[2]{0:T(128)} %cnt_hbm.1), custom_call_target="tpu_custom_call" | custom-call | tf_op jit(solution)/shard_map/pallas_call | solution.py:301
  31.8 0.6 %shard_map.51 = (bf16[128,128]{1,0:T(8,128)(2,1)}, f32[2,128]{1,0:T(2,128)}) custom-call(bf16[128,128]{1,0:T(8,128)(2,1)S(1)} %get-tuple-element.4.stat_ref, f32[2,128]{1,0:T(2,128)S(1)} %get-tuple-element.5.exc_ref), custom_call_target="tpu_custom_call" | custom-call | tf_op jit(solution)/shard_map/pallas_call | solution.py:343

commit v4 on v3

--- a/solution.py
+++ b/solution.py
@@ -152,6 +152,20 @@
             ).start()
     pltpu.make_async_copy(note, heard.at[0, q], heard_sem.at[0]).start()
 
+    def give(k, to_seg, which):
+        for i in range(*waves[k]):
+            slice_ids = range(SUB) if which else [s for s, _ in peers(i)]
+            for s in slice_ids:
+                pltpu.make_async_remote_copy(
+                    src_ref=rows_out.at[i, s],
+                    dst_ref=rows_in.at[group, lat],
+                    send_sem=rows_send.at[which],
+                    recv_sem=rows_sem.at[group],
+                    device_id=(to_seg, first_at[i] + s),
+                    device_id_type=MESH,
+                ).start()
+
+    held = half // 2
     load.wait()
     bin_id = lax.broadcasted_iota(i32, (1, bins), 1).astype(f32)
     total_sum = jnp.zeros((1, width), f32)
@@ -179,23 +193,14 @@
         rows_out[lo:hi] = rows.reshape(hi - lo, SUB, slots, width)
         if k == 0:
             wait_bytes(pair_note, pair_sem)
-
-        for i in range(lo, hi):
-            targets = [(other_seg, s, first_at[i] + s, 1) for s in range(SUB)]
-            targets += [(seg, s, d, 0) for s, d in peers(i)]
-            for g, s, d, which in targets:
-                pltpu.make_async_remote_copy(
-                    src_ref=rows_out.at[i, s],
-                    dst_ref=rows_in.at[group, lat],
-                    send_sem=rows_send.at[which],
-                    recv_sem=rows_sem.at[group],
-                    device_id=(g, d),
-                    device_id_type=MESH,
-                ).start()
-            if i == 0:
-                pltpu.make_async_copy(
-                    rows_out.at[0, q], rows_in.at[group, lat], rows_sem.at[group]
-                ).start()
+            pltpu.make_async_copy(
+                rows_out.at[0, q], rows_in.at[group, lat], rows_sem.at[group]
+            ).start()
+        if k != held:
+            give(k, other_seg, 1)
+        give(k, seg, 0)
+        if k == len(waves) - 1:
+            give(held, other_seg, 1)
         total_sum += jnp.sum(jnp.where(is_valid, rows, 0.0), axis=0, keepdims=True)
         total_count += jnp.sum(valid, keepdims=True)
 

time: 32.6 us -> 32.5 us (level)
  no operation moved by 1% of the time
where the time goes in v4:
time: 32.5 us; the launch traced here: 32.4 us
  Pallas kernels  31.7 us (98%)
  between operations  0.64 us (2%)
    pallas_call x1, Pallas kernels, shards(): pl.pallas_call(functools.partial(kernel, n_seg, n_lat), out_shape=(pltpu....  31.1 us

profile of v4, /device:TPU:1, one launch (start us, length us, event | category | flops | bytes accessed | tf_op | source)
XLA Modules:
  0.0 32.4 jit_solution(11751317298837068022)
XLA Ops:
  0.6 31.1 %shard_map.50 = (bf16[128,128]{1,0:T(8,128)(2,1)S(1)}, f32[2,128]{1,0:T(2,128)S(1)}) custom-call(bf16[1,2048,128]{2,1,0:T(8,128)(2,1)} %map_ref.1, s32[1,128]{1,0:T(1,128)} %pos_hbm.1, s32[2]{0:T(128)} %cnt_hbm.1), custom_call_target="tpu_custom_call" | custom-call | tf_op jit(solution)/shard_map/pallas_call | solution.py:306
  31.7 0.6 %shard_map.51 = (bf16[128,128]{1,0:T(8,128)(2,1)}, f32[2,128]{1,0:T(2,128)}) custom-call(bf16[128,128]{1,0:T(8,128)(2,1)S(1)} %get-tuple-element.4.stat_ref, f32[2,128]{1,0:T(2,128)S(1)} %get-tuple-element.5.exc_ref), custom_call_target="tpu_custom_call" | custom-call | tf_op jit(solution)/shard_map/pallas_call | solution.py:348

commit v5 on v4

--- a/solution.py
+++ b/solution.py
@@ -113,19 +113,23 @@
         1.0,
         0.0,
     ).astype(bf16)
+    hs = slots // 2
     dest_id = lax.broadcasted_iota(i32, (n_lat, points), 0)
-    flat_id = lax.broadcasted_iota(i32, (n_lat * slots, points), 0).astype(f32)
-
-    def chooser(positions):
+    flat_id = lax.broadcasted_iota(i32, (n_lat * hs, points), 0).astype(f32)
+
+    def choose(g, positions):
         dest = lax.div(positions, span)
         at_dest = jnp.where(dest == dest_id, 1.0, 0.0)
         ahead = jnp.dot(at_dest.astype(bf16), before_mat, preferred_element_type=f32)
         slot = jnp.sum(at_dest * ahead, axis=0, keepdims=True)
-        flat = dest.astype(f32) * slots + slot
-        return jnp.where(flat_id == flat, 1.0, 0.0).T.astype(bf16)
+        base = dest.astype(f32) * hs + slot
+        flat_low = jnp.where(slot < hs, base, -1.0)
+        flat_high = jnp.where(slot < hs, -1.0, base - hs)
+        pick[g, 0:points] = jnp.where(flat_id == flat_low, 1.0, 0.0).T.astype(bf16)
+        pick[g, points : 2 * points] = jnp.where(flat_id == flat_high, 1.0, 0.0).T.astype(bf16)
 
     load_pos.wait()
-    pick[group] = chooser(note[0:1, :])
+    choose(group, note[0:1, :])
 
     pl.semaphore_wait(barrier, n_lat - 1 + 1 + n_y - 1)
 
@@ -152,20 +156,34 @@
             ).start()
     pltpu.make_async_copy(note, heard.at[0, q], heard_sem.at[0]).start()
 
-    def give(k, to_seg, which):
+    def give(k, h):
         for i in range(*waves[k]):
-            slice_ids = range(SUB) if which else [s for s, _ in peers(i)]
-            for s in slice_ids:
+            targets = [(other_seg, s, first_at[i] + s, 1) for s in range(SUB)]
+            targets += [(seg, s, d, 0) for s, d in peers(i)]
+            for to_seg, s, d, which in targets:
                 pltpu.make_async_remote_copy(
-                    src_ref=rows_out.at[i, s],
-                    dst_ref=rows_in.at[group, lat],
-                    send_sem=rows_send.at[which],
-                    recv_sem=rows_sem.at[group],
-                    device_id=(to_seg, first_at[i] + s),
+                    src_ref=rows_out.at[h, i, s],
+                    dst_ref=rows_in.at[h, group, lat],
+                    send_sem=rows_send.at[h, which],
+                    recv_sem=rows_sem.at[h, group],
+                    device_id=(to_seg, d),
                     device_id_type=MESH,
                 ).start()
-
-    held = half // 2
+            if i == 0:
+                pltpu.make_async_copy(
+                    rows_out.at[h, 0, q], rows_in.at[h, group, lat], rows_sem.at[h, group]
+                ).start()
+
+    order = [[(k, 0), (k, 1)] for k in range(len(waves))]
+    order[2] = [(2, 0)]
+    order[3] = [(3, 0)]
+    order[4] = [(4, 0), (3, 1), (4, 1), (2, 1)]
+    tile = (1, slots, width)
+    upper = lax.broadcasted_iota(i32, tile, 1) >= hs
+    right = lax.broadcasted_iota(i32, tile, 2) >= width // 2
+    stays = upper == right
+    on_left = lax.broadcasted_iota(i32, (1, width), 1) < width // 2
+
     load.wait()
     bin_id = lax.broadcasted_iota(i32, (1, bins), 1).astype(f32)
     total_sum = jnp.zeros((1, width), f32)
@@ -190,17 +208,15 @@
         at_bin = code - jnp.where(is_valid, VALID + LIVE, LIVE)
         weights = jnp.maximum(1.0 - jnp.abs(at_bin - bin_id), 0.0).astype(bf16)
         rows = jnp.dot(weights, table[...], preferred_element_type=f32)
-        rows_out[lo:hi] = rows.reshape(hi - lo, SUB, slots, width)
+        tiles = rows.reshape(n, slots, width)
+        swapped = pltpu.roll(pltpu.roll(tiles, hs, 1), width // 2, 2)
+        tiles = jnp.where(stays, tiles, swapped).reshape(hi - lo, SUB, slots, width)
+        rows_out[0, lo:hi] = tiles[:, :, 0:hs]
+        rows_out[1, lo:hi] = tiles[:, :, hs:slots]
         if k == 0:
             wait_bytes(pair_note, pair_sem)
-            pltpu.make_async_copy(
-                rows_out.at[0, q], rows_in.at[group, lat], rows_sem.at[group]
-            ).start()
-        if k != held:
-            give(k, other_seg, 1)
-        give(k, seg, 0)
-        if k == len(waves) - 1:
-            give(held, other_seg, 1)
+        for w, h in order[k]:
+            give(w, h)
         total_sum += jnp.sum(jnp.where(is_valid, rows, 0.0), axis=0, keepdims=True)
         total_count += jnp.sum(valid, keepdims=True)
 
@@ -218,7 +234,7 @@
             device_id_type=MESH,
         ).start()
 
-    pick[other] = chooser(pair_note[0:1, :])
+    choose(other, pair_note[0:1, :])
 
     wait_bytes(near_in.at[0 : PAIR * SUB - 1], near_sem)
     near_sum = jnp.sum(near_in[...], axis=0)
@@ -234,41 +250,56 @@
             device_id_type=MESH,
         ).start()
 
-    own = jnp.zeros((points, width), f32)
-    for g in range(PAIR):
-        wait_bytes(rows_in.at[g], rows_sem.at[g])
-        got = rows_in[g].reshape(n_lat * slots, width)
-        high = got.astype(bf16)
-        rest = got - high.astype(f32)
-        mid = rest.astype(bf16)
-        low = (rest - mid.astype(f32)).astype(bf16)
-        choice = pick[g]
-        own += (
-            jnp.dot(choice, low, preferred_element_type=f32)
-            + jnp.dot(choice, mid, preferred_element_type=f32)
-            + jnp.dot(choice, high, preferred_element_type=f32)
+    turn = functools.partial(pltpu.roll, shift=width // 2, axis=1)
+    hp = points // 2
+    for h in range(2):
+        both = jnp.zeros((2 * points, width), f32)
+        for g in range(PAIR):
+            wait_bytes(rows_in.at[h, g], rows_sem.at[h, g])
+            got = rows_in[h, g].reshape(n_lat * hs, width)
+            high = got.astype(bf16)
+            mid = (got - high.astype(f32)).astype(bf16)
+            choice = pick[g]
+            both += jnp.dot(choice, mid, preferred_element_type=f32)
+            both += jnp.dot(choice, high, preferred_element_type=f32)
+        part[h, y, 0:hp, :] = jnp.where(
+            on_left,
+            both[0:hp] + turn(both[points : points + hp]),
+            turn(both[hp:points]) + both[points + hp : 2 * points],
         )
-    part[y, 0:points, :] = own
-    wait_bytes(far_in.at[0 : n_z - 1], far_sem)
-    part[y, points : points + 8, :] = jnp.broadcast_to(jnp.sum(far_in[...], axis=0), (8, width))
-
-    for peer in y_peers[1:] + y_peers[:1]:
-        pltpu.make_async_remote_copy(
-            src_ref=part.at[y],
-            dst_ref=part.at[y],
-            send_sem=part_send,
-            recv_sem=part_sem,
-            device_id=(peer, lat),
-            device_id_type=MESH,
-        ).start()
-    wait_bytes(part.at[0 : n_y - 1], part_sem)
-
-    all_sum = part[0]
-    for k in range(1, n_y):
-        all_sum = all_sum + part[k]
-    stat = all_sum[0:points] * (1.0 / n_seg)
+        if h == 1:
+            wait_bytes(far_in.at[0 : n_z - 1], far_sem)
+            part[h, y, hp : hp + 8, :] = jnp.broadcast_to(
+                jnp.sum(far_in[...], axis=0), (8, width)
+            )
+        length = hp + 8 * h
+
+        for peer in y_peers[1:] + y_peers[:1]:
+            pltpu.make_async_remote_copy(
+                src_ref=part.at[h, y, 0:length],
+                dst_ref=part.at[h, y, 0:length],
+                send_sem=part_send.at[h],
+                recv_sem=part_sem.at[h],
+                device_id=(peer, lat),
+                device_id_type=MESH,
+            ).start()
+
+    sums = []
+    for h in range(2):
+        length = hp + 8 * h
+        wait_bytes(part.at[h, 0 : n_y - 1, 0:length], part_sem.at[h])
+        whole = part[h, 0, 0:length]
+        for k in range(1, n_y):
+            whole = whole + part[h, k, 0:length]
+        sums.append(whole)
+    left, right_ = sums[0], sums[1][0:hp]
+    all_sum = jnp.concatenate(
+        [jnp.where(on_left, left, turn(right_)), jnp.where(on_left, turn(left), right_)], axis=0
+    )
+    valid_total = sums[1][hp : hp + 1]
+    stat = all_sum * (1.0 / n_seg)
     stat_ref[...] = stat.astype(bf16)
-    global_mean = all_sum[points : points + 1] * (1.0 / n_seg) / total_count
+    global_mean = valid_total * (1.0 / n_seg) / total_count
     row_id = lax.broadcasted_iota(i32, (block_size, width), 0)
     for b in range(blocks):
         count = cnt_ref[b]
@@ -277,11 +308,12 @@
         exc_ref[b : b + 1, :] = block_sum / count.astype(f32) - global_mean
 
     wait_bytes(heard, note_send)
-    wait_bytes(rows_in.at[0, 0 : n_lat - 1], rows_send.at[0])
-    wait_bytes(rows_in.at[0], rows_send.at[1])
+    for h in range(2):
+        wait_bytes(rows_in.at[h, 0, 0 : n_lat - 1], rows_send.at[h, 0])
+        wait_bytes(rows_in.at[h, 1], rows_send.at[h, 1])
+        wait_bytes(part.at[h, 0 : n_y - 1, 0 : hp + 8 * h], part_send.at[h])
     wait_bytes(near_in.at[0 : PAIR * SUB - 1], sum_send.at[0])
     wait_bytes(far_in.at[0 : n_z - 1], sum_send.at[1])
-    wait_bytes(part.at[0 : n_y - 1], part_send)
 
 
 def put_out(stat_ref, exc_ref, stat_out, exc_out, stat_sem, exc_sem):
@@ -321,26 +353,26 @@
             pltpu.VMEM((2, points), jnp.int32),
             pltpu.VMEM((n_z, SUB, 2, points), jnp.int32),
             pltpu.VMEM((2, points), jnp.int32),
-            pltpu.VMEM((n_z, SUB, slots, width), jnp.float32),
-            pltpu.VMEM((PAIR, n_lat, slots, width), jnp.float32),
+            pltpu.VMEM((2, n_z, SUB, slots // 2, width), jnp.float32),
+            pltpu.VMEM((2, PAIR, n_lat, slots // 2, width), jnp.float32),
             pltpu.VMEM((2, 1, width), jnp.float32),
             pltpu.VMEM((PAIR * SUB, 1, width), jnp.float32),
             pltpu.VMEM((n_z, 1, width), jnp.float32),
-            pltpu.VMEM((PAIR, points, n_lat * slots), jnp.bfloat16),
-            pltpu.VMEM((n_y, points + 8, width), jnp.float32),
+            pltpu.VMEM((PAIR, 2 * points, n_lat * slots // 2), jnp.bfloat16),
+            pltpu.VMEM((2, n_y, points // 2 + 8, width), jnp.float32),
             dma,
             dma,
             dma,
             dma,
             dma((n_z // 2 + 1,)),
             dma,
+            dma((2, 2)),
+            dma((2, PAIR)),
             dma((2,)),
-            dma((PAIR,)),
+            dma,
+            dma,
             dma((2,)),
-            dma,
-            dma,
-            dma,
-            dma,
+            dma((2,)),
         ],
         compiler_params=pltpu.CompilerParams(collective_id=0, has_side_effects=True),
     )(coh_map, positions, counts)

time: 32.5 us -> 30.9 us (0.951)
  Pallas kernels: 31.7 us -> 30.1 us
    pallas_call x1, Pallas kernels: 31.1 us -> 29.5 us  [shards(): pl.pallas_call(functools.partial(kernel, n_seg, n_lat), out_shape=(pltpu....]
where the time goes in v5:
time: 30.9 us; the launch traced here: 30.8 us
  Pallas kernels  30.1 us (97%)
  between operations  0.64 us (2%)
    pallas_call x1, Pallas kernels, shards(): pl.pallas_call(functools.partial(kernel, n_seg, n_lat), out_shape=(pltpu....  29.5 us
    pallas_call x1, Pallas kernels, shards(): pl.pallas_call(put_out, out_shape=(jax.ShapeDtypeStruct((points, width),...  0.64 us

profile of v5, /device:TPU:1, one launch (start us, length us, event | category | flops | bytes accessed | tf_op | source)
XLA Modules:
  0.0 30.8 jit_solution(16689475514627911257)
XLA Ops:
  0.6 29.5 %shard_map.50 = (bf16[128,128]{1,0:T(8,128)(2,1)S(1)}, f32[2,128]{1,0:T(2,128)S(1)}) custom-call(bf16[1,2048,128]{2,1,0:T(8,128)(2,1)} %map_ref.1, s32[1,128]{1,0:T(1,128)} %pos_hbm.1, s32[2]{0:T(128)} %cnt_hbm.1), custom_call_target="tpu_custom_call" | custom-call | tf_op jit(solution)/shard_map/pallas_call | solution.py:338
  30.1 0.6 %shard_map.51 = (bf16[128,128]{1,0:T(8,128)(2,1)}, f32[2,128]{1,0:T(2,128)}) custom-call(bf16[128,128]{1,0:T(8,128)(2,1)S(1)} %get-tuple-element.4.stat_ref, f32[2,128]{1,0:T(2,128)S(1)} %get-tuple-element.5.exc_ref), custom_call_target="tpu_custom_call" | custom-call | tf_op jit(solution)/shard_map/pallas_call | solution.py:380

commit v6 on v5

--- a/solution.py
+++ b/solution.py
@@ -36,6 +36,7 @@
     rows_in,
     sum_out,
     near_in,
+    mid_in,
     far_in,
     pick,
     part,
@@ -49,6 +50,7 @@
     rows_sem,
     sum_send,
     near_sem,
+    mid_sem,
     far_sem,
     part_send,
     part_sem,
@@ -79,9 +81,9 @@
     def peers(i):
         if i == 0:
             return [(nq, first_at[0] + nq) for nq in near_q]
-        return [(s, first_at[i] + s) for s in range(SUB)]
-
-    y_peers = [group * n_y + lax.rem(y + k, n_y) for k in range(1, n_y)]
+        return [(s, first_at[i] + s) for s in (1, 3, 2, 0)]
+
+    y_peers = [group * n_y + k + jnp.where(y <= k, 1, 0) for k in range(n_y - 1)]
     far_first = list(range(n_z - 1, -1, -1))
 
     load_pos = pltpu.make_async_copy(pos_hbm, note.at[0:1], pos_sem)
@@ -156,28 +158,33 @@
             ).start()
     pltpu.make_async_copy(note, heard.at[0, q], heard_sem.at[0]).start()
 
-    def give(k, h):
-        for i in range(*waves[k]):
-            targets = [(other_seg, s, first_at[i] + s, 1) for s in range(SUB)]
-            targets += [(seg, s, d, 0) for s, d in peers(i)]
-            for to_seg, s, d, which in targets:
-                pltpu.make_async_remote_copy(
-                    src_ref=rows_out.at[h, i, s],
-                    dst_ref=rows_in.at[h, group, lat],
-                    send_sem=rows_send.at[h, which],
-                    recv_sem=rows_sem.at[h, group],
-                    device_id=(to_seg, d),
-                    device_id_type=MESH,
-                ).start()
-            if i == 0:
-                pltpu.make_async_copy(
-                    rows_out.at[h, 0, q], rows_in.at[h, group, lat], rows_sem.at[h, group]
-                ).start()
-
-    order = [[(k, 0), (k, 1)] for k in range(len(waves))]
-    order[2] = [(2, 0)]
-    order[3] = [(3, 0)]
-    order[4] = [(4, 0), (3, 1), (4, 1), (2, 1)]
+    def give(i, h):
+        if i == 0:
+            targets = [(seg, s, d, 0) for s, d in peers(0)]
+            targets += [(other_seg, s, first_at[0] + s, 1) for s in range(SUB)]
+        else:
+            targets = [
+                (g * n_y + y, s, d, lax.rem(group + g, PAIR))
+                for g in range(PAIR)
+                for s, d in peers(i)
+            ]
+        for to_seg, s, d, which in targets:
+            pltpu.make_async_remote_copy(
+                src_ref=rows_out.at[h, i, s],
+                dst_ref=rows_in.at[h, group, lat],
+                send_sem=rows_send.at[h, which],
+                recv_sem=rows_sem.at[h, group],
+                device_id=(to_seg, d),
+                device_id_type=MESH,
+            ).start()
+        if i == 0:
+            pltpu.make_async_copy(
+                rows_out.at[h, 0, q], rows_in.at[h, group, lat], rows_sem.at[h, group]
+            ).start()
+
+    order = [[], [((1, 2), 0, ""), ((1, 2), 1, "e")], [((3, 4), 0, "")], [((5, 6), 0, "e")], [((7,), 0, "e"), ((5, 6), 0, "l"), ((7,), 0, "l"), ((5, 6, 7), 1, "e"), ((3, 4), 1, "e"), ((5, 6, 7, 3, 4, 1, 2), 1, "l")]]
+    early = [first_at[i] < half * SUB for i in range(n_z)]
+
     tile = (1, slots, width)
     upper = lax.broadcasted_iota(i32, tile, 1) >= hs
     right = lax.broadcasted_iota(i32, tile, 2) >= width // 2
@@ -215,37 +222,48 @@
         rows_out[1, lo:hi] = tiles[:, :, hs:slots]
         if k == 0:
             wait_bytes(pair_note, pair_sem)
-        for w, h in order[k]:
-            give(w, h)
         total_sum += jnp.sum(jnp.where(is_valid, rows, 0.0), axis=0, keepdims=True)
         total_count += jnp.sum(valid, keepdims=True)
 
-    sum_out[0] = total_sum
-    near_in[group * SUB + q] = total_sum
-    for g, d in [(other_seg, first_at[0] + s) for s in range(SUB)] + [
-        (seg, d) for _, d in peers(0)
-    ]:
-        pltpu.make_async_remote_copy(
-            src_ref=sum_out.at[0],
-            dst_ref=near_in.at[group * SUB + q],
-            send_sem=sum_send.at[0],
-            recv_sem=near_sem,
-            device_id=(g, d),
-            device_id_type=MESH,
-        ).start()
+        if k == len(waves) - 1:
+            sum_out[0] = total_sum
+            near_in[group * SUB + q] = total_sum
+            for g, d in [(other_seg, first_at[0] + s) for s in range(SUB)] + [
+                (seg, d) for _, d in peers(0)
+            ]:
+                pltpu.make_async_remote_copy(
+                    src_ref=sum_out.at[0],
+                    dst_ref=near_in.at[group * SUB + q],
+                    send_sem=sum_send.at[0],
+                    recv_sem=near_sem,
+                    device_id=(g, d),
+                    device_id_type=MESH,
+                ).start()
+
+        if k == 0:
+            give(0, 0)
+            give(0, 1)
+        for ids, h, cond in order[k]:
+            for i in ids:
+                if cond == "e":
+                    pl.when(early[i])(functools.partial(give, i, h))
+                elif cond == "l":
+                    pl.when(jnp.logical_not(early[i]))(functools.partial(give, i, h))
+                else:
+                    give(i, h)
 
     choose(other, pair_note[0:1, :])
 
     wait_bytes(near_in.at[0 : PAIR * SUB - 1], near_sem)
     near_sum = jnp.sum(near_in[...], axis=0)
     sum_out[1] = near_sum
-    far_in[z] = near_sum
-    for i in far_first[:-1]:
+    mid_in[z] = near_sum
+    for i in range(1, n_z):
         pltpu.make_async_remote_copy(
             src_ref=sum_out.at[1],
-            dst_ref=far_in.at[z],
+            dst_ref=mid_in.at[z],
             send_sem=sum_send.at[1],
-            recv_sem=far_sem,
+            recv_sem=mid_sem,
             device_id=(seg, first_at[i] + q),
             device_id_type=MESH,
         ).start()
@@ -262,41 +280,50 @@
             choice = pick[g]
             both += jnp.dot(choice, mid, preferred_element_type=f32)
             both += jnp.dot(choice, high, preferred_element_type=f32)
-        part[h, y, 0:hp, :] = jnp.where(
+        part[h, y] = jnp.where(
             on_left,
             both[0:hp] + turn(both[points : points + hp]),
             turn(both[hp:points]) + both[points + hp : 2 * points],
         )
-        if h == 1:
-            wait_bytes(far_in.at[0 : n_z - 1], far_sem)
-            part[h, y, hp : hp + 8, :] = jnp.broadcast_to(
-                jnp.sum(far_in[...], axis=0), (8, width)
-            )
-        length = hp + 8 * h
-
-        for peer in y_peers[1:] + y_peers[:1]:
+
+        for peer in y_peers:
             pltpu.make_async_remote_copy(
-                src_ref=part.at[h, y, 0:length],
-                dst_ref=part.at[h, y, 0:length],
+                src_ref=part.at[h, y],
+                dst_ref=part.at[h, y],
                 send_sem=part_send.at[h],
                 recv_sem=part_sem.at[h],
                 device_id=(peer, lat),
                 device_id_type=MESH,
             ).start()
 
+        if h == 1:
+            wait_bytes(mid_in.at[0 : n_z - 1], mid_sem)
+            mid_sum = jnp.sum(mid_in[...], axis=0)
+            sum_out[2] = mid_sum
+            far_in[y] = mid_sum
+            for peer in y_peers:
+                pltpu.make_async_remote_copy(
+                    src_ref=sum_out.at[2],
+                    dst_ref=far_in.at[y],
+                    send_sem=sum_send.at[2],
+                    recv_sem=far_sem,
+                    device_id=(peer, lat),
+                    device_id_type=MESH,
+                ).start()
+
     sums = []
     for h in range(2):
-        length = hp + 8 * h
-        wait_bytes(part.at[h, 0 : n_y - 1, 0:length], part_sem.at[h])
-        whole = part[h, 0, 0:length]
+        wait_bytes(part.at[h, 0 : n_y - 1], part_sem.at[h])
+        whole = part[h, 0]
         for k in range(1, n_y):
-            whole = whole + part[h, k, 0:length]
+            whole = whole + part[h, k]
         sums.append(whole)
-    left, right_ = sums[0], sums[1][0:hp]
+    left, right_ = sums[0], sums[1]
     all_sum = jnp.concatenate(
         [jnp.where(on_left, left, turn(right_)), jnp.where(on_left, turn(left), right_)], axis=0
     )
-    valid_total = sums[1][hp : hp + 1]
+    wait_bytes(far_in.at[0 : n_y - 1], far_sem)
+    valid_total = jnp.sum(far_in[...], axis=0)
     stat = all_sum * (1.0 / n_seg)
     stat_ref[...] = stat.astype(bf16)
     global_mean = valid_total * (1.0 / n_seg) / total_count
@@ -311,9 +338,10 @@
     for h in range(2):
         wait_bytes(rows_in.at[h, 0, 0 : n_lat - 1], rows_send.at[h, 0])
         wait_bytes(rows_in.at[h, 1], rows_send.at[h, 1])
-        wait_bytes(part.at[h, 0 : n_y - 1, 0 : hp + 8 * h], part_send.at[h])
+        wait_bytes(part.at[h, 0 : n_y - 1], part_send.at[h])
     wait_bytes(near_in.at[0 : PAIR * SUB - 1], sum_send.at[0])
-    wait_bytes(far_in.at[0 : n_z - 1], sum_send.at[1])
+    wait_bytes(mid_in.at[0 : n_z - 1], sum_send.at[1])
+    wait_bytes(far_in.at[0 : n_y - 1], sum_send.at[2])
 
 
 def put_out(stat_ref, exc_ref, stat_out, exc_out, stat_sem, exc_sem):
@@ -355,11 +383,12 @@
             pltpu.VMEM((2, points), jnp.int32),
             pltpu.VMEM((2, n_z, SUB, slots // 2, width), jnp.float32),
             pltpu.VMEM((2, PAIR, n_lat, slots // 2, width), jnp.float32),
-            pltpu.VMEM((2, 1, width), jnp.float32),
+            pltpu.VMEM((3, 1, width), jnp.float32),
             pltpu.VMEM((PAIR * SUB, 1, width), jnp.float32),
             pltpu.VMEM((n_z, 1, width), jnp.float32),
+            pltpu.VMEM((n_y, 1, width), jnp.float32),
             pltpu.VMEM((PAIR, 2 * points, n_lat * slots // 2), jnp.bfloat16),
-            pltpu.VMEM((2, n_y, points // 2 + 8, width), jnp.float32),
+            pltpu.VMEM((2, n_y, points // 2, width), jnp.float32),
             dma,
             dma,
             dma,
@@ -368,7 +397,8 @@
             dma,
             dma((2, 2)),
             dma((2, PAIR)),
-            dma((2,)),
+            dma((3,)),
+            dma,
             dma,
             dma,
             dma((2,)),

time: 30.9 us -> 30.1 us (0.974)
  Pallas kernels: 30.1 us -> 29.4 us
    pallas_call x1, Pallas kernels: 29.5 us -> 28.8 us  [shards(): pl.pallas_call(functools.partial(kernel, n_seg, n_lat), out_shape=(pltpu....]
where the time goes in v6:
time: 30.1 us; the launch traced here: 30 us
  Pallas kernels  29.4 us (98%)
  between operations  0.64 us (2%)
    pallas_call x1, Pallas kernels, shards(): pl.pallas_call(functools.partial(kernel, n_seg, n_lat), out_shape=(pltpu....  28.8 us
    pallas_call x1, Pallas kernels, shards(): pl.pallas_call(put_out, out_shape=(jax.ShapeDtypeStruct((points, width),...  0.64 us

profile of v6, /device:TPU:1, one launch (start us, length us, event | category | flops | bytes accessed | tf_op | source)
XLA Modules:
  0.0 30.0 jit_solution(14430040514451925845)
XLA Ops:
  0.6 28.8 %shard_map.50 = (bf16[128,128]{1,0:T(8,128)(2,1)S(1)}, f32[2,128]{1,0:T(2,128)S(1)}) custom-call(bf16[1,2048,128]{2,1,0:T(8,128)(2,1)} %map_ref.1, s32[1,128]{1,0:T(1,128)} %pos_hbm.1, s32[2]{0:T(128)} %cnt_hbm.1), custom_call_target="tpu_custom_call" | custom-call | tf_op jit(solution)/shard_map/pallas_call | solution.py:366
  29.4 0.6 %shard_map.51 = (bf16[128,128]{1,0:T(8,128)(2,1)}, f32[2,128]{1,0:T(2,128)}) custom-call(bf16[128,128]{1,0:T(8,128)(2,1)S(1)} %get-tuple-element.4.stat_ref, f32[2,128]{1,0:T(2,128)S(1)} %get-tuple-element.5.exc_ref), custom_call_target="tpu_custom_call" | custom-call | tf_op jit(solution)/shard_map/pallas_call | solution.py:410

commit v7 on v6

--- a/solution.py
+++ b/solution.py
@@ -48,11 +48,9 @@
     pair_sem,
     rows_send,
     rows_sem,
-    sum_send,
     near_sem,
     mid_sem,
     far_sem,
-    part_send,
     part_sem,
 ):
     n_y = n_seg // PAIR
@@ -127,11 +125,15 @@
         base = dest.astype(f32) * hs + slot
         flat_low = jnp.where(slot < hs, base, -1.0)
         flat_high = jnp.where(slot < hs, -1.0, base - hs)
-        pick[g, 0:points] = jnp.where(flat_id == flat_low, 1.0, 0.0).T.astype(bf16)
-        pick[g, points : 2 * points] = jnp.where(flat_id == flat_high, 1.0, 0.0).T.astype(bf16)
+        depth = n_lat * hs
+        for h, flat in enumerate((flat_low, flat_high)):
+            choice = jnp.where(flat_id == flat, 1.0, 0.0).T.astype(bf16)
+            for c in range(2):
+                pick[g, h * points : (h + 1) * points, c * depth : (c + 1) * depth] = choice
+        return slot
 
     load_pos.wait()
-    choose(group, note[0:1, :])
+    note[2:3, :] = choose(group, note[0:1, :]).astype(i32)
 
     pl.semaphore_wait(barrier, n_lat - 1 + 1 + n_y - 1)
 
@@ -160,29 +162,31 @@
 
     def give(i, h):
         if i == 0:
-            targets = [(seg, s, d, 0) for s, d in peers(0)]
-            targets += [(other_seg, s, first_at[0] + s, 1) for s in range(SUB)]
+            targets = [(seg, s, d) for s, d in peers(0)]
+            targets += [(other_seg, s, first_at[0] + s) for s in range(SUB)]
         else:
             targets = [
-                (g * n_y + y, s, d, lax.rem(group + g, PAIR))
+                (g * n_y + y, s, d)
                 for g in range(PAIR)
                 for s, d in peers(i)
             ]
-        for to_seg, s, d, which in targets:
+        for to_seg, s, d in targets:
             pltpu.make_async_remote_copy(
                 src_ref=rows_out.at[h, i, s],
-                dst_ref=rows_in.at[h, group, lat],
-                send_sem=rows_send.at[h, which],
+                dst_ref=rows_in.at[(h * PAIR + group) * n_lat + lat],
+                send_sem=rows_send,
                 recv_sem=rows_sem.at[h, group],
                 device_id=(to_seg, d),
                 device_id_type=MESH,
             ).start()
         if i == 0:
             pltpu.make_async_copy(
-                rows_out.at[h, 0, q], rows_in.at[h, group, lat], rows_sem.at[h, group]
+                rows_out.at[h, 0, q],
+                rows_in.at[(h * PAIR + group) * n_lat + lat],
+                rows_sem.at[h, group],
             ).start()
 
-    order = [[], [((1, 2), 0, ""), ((1, 2), 1, "e")], [((3, 4), 0, "")], [((5, 6), 0, "e")], [((7,), 0, "e"), ((5, 6), 0, "l"), ((7,), 0, "l"), ((5, 6, 7), 1, "e"), ((3, 4), 1, "e"), ((5, 6, 7, 3, 4, 1, 2), 1, "l")]]
+    order = [[], [((1, 2), 0, ""), ((1, 2), 1, "e")], [((3, 4), 0, "")], [((5, 6), 0, "e")], [((7,), 0, "e"), ((5, 6, 7), 1, "e"), ((3, 4), 1, "e"), ((5, 6, 7), 0, "l"), ((5, 6, 7, 3, 4, 1, 2), 1, "l")]]
     early = [first_at[i] < half * SUB for i in range(n_z)]
 
     tile = (1, slots, width)
@@ -202,10 +206,8 @@
         ok = heard[lo:hi, :, 1, :].reshape(n, points)
         rel = pos - lat * span
         hit = (rel >= 0) & (rel < span)
-        before = jnp.dot(
-            jnp.where(hit, 1.0, 0.0).astype(bf16), before_mat, preferred_element_type=f32
-        )
-        key = jnp.where(hit, before, -1.0)
+        rank = heard[lo:hi, :, 2, :].reshape(n, points)
+        key = jnp.where(hit, rank.astype(f32), -1.0)
         valid = ok.astype(f32)
         coded = jnp.where(hit, rel.astype(f32) * (1.0 / PER_BIN) + LIVE + valid * VALID, 0.0)
         slot_id = lax.broadcasted_iota(i32, (n, slots, points), 1).astype(f32)
@@ -234,7 +236,7 @@
                 pltpu.make_async_remote_copy(
                     src_ref=sum_out.at[0],
                     dst_ref=near_in.at[group * SUB + q],
-                    send_sem=sum_send.at[0],
+                    send_sem=pos_sem,
                     recv_sem=near_sem,
                     device_id=(g, d),
                     device_id_type=MESH,
@@ -262,25 +264,26 @@
         pltpu.make_async_remote_copy(
             src_ref=sum_out.at[1],
             dst_ref=mid_in.at[z],
-            send_sem=sum_send.at[1],
+            send_sem=cnt_sem,
             recv_sem=mid_sem,
             device_id=(seg, first_at[i] + q),
             device_id_type=MESH,
         ).start()
 
+    wait_bytes(heard, note_send)
     turn = functools.partial(pltpu.roll, shift=width // 2, axis=1)
     hp = points // 2
     for h in range(2):
         both = jnp.zeros((2 * points, width), f32)
         for g in range(PAIR):
-            wait_bytes(rows_in.at[h, g], rows_sem.at[h, g])
-            got = rows_in[h, g].reshape(n_lat * hs, width)
+            lo = (h * PAIR + g) * n_lat
+            wait_bytes(rows_in.at[lo : lo + n_lat], rows_sem.at[h, g])
+            got = rows_in[lo : lo + n_lat].reshape(n_lat * hs, width)
             high = got.astype(bf16)
             mid = (got - high.astype(f32)).astype(bf16)
-            choice = pick[g]
-            both += jnp.dot(choice, mid, preferred_element_type=f32)
-            both += jnp.dot(choice, high, preferred_element_type=f32)
-        part[h, y] = jnp.where(
+            terms = jnp.concatenate([high, mid], axis=0)
+            both += jnp.dot(pick[g], terms, preferred_element_type=f32)
+        part[h * n_y + y] = jnp.where(
             on_left,
             both[0:hp] + turn(both[points : points + hp]),
             turn(both[hp:points]) + both[points + hp : 2 * points],
@@ -288,9 +291,9 @@
 
         for peer in y_peers:
             pltpu.make_async_remote_copy(
-                src_ref=part.at[h, y],
-                dst_ref=part.at[h, y],
-                send_sem=part_send.at[h],
+                src_ref=part.at[h * n_y + y],
+                dst_ref=part.at[h * n_y + y],
+                send_sem=note_send,
                 recv_sem=part_sem.at[h],
                 device_id=(peer, lat),
                 device_id_type=MESH,
@@ -305,18 +308,23 @@
                 pltpu.make_async_remote_copy(
                     src_ref=sum_out.at[2],
                     dst_ref=far_in.at[y],
-                    send_sem=sum_send.at[2],
+                    send_sem=table_sem,
                     recv_sem=far_sem,
                     device_id=(peer, lat),
                     device_id_type=MESH,
                 ).start()
 
+    wait_bytes(rows_in.at[0 : 2 * (PAIR * n_lat - 1)], rows_send)
+    wait_bytes(near_in.at[0 : PAIR * SUB - 1], pos_sem)
+    wait_bytes(mid_in.at[0 : n_z - 1], cnt_sem)
+    wait_bytes(far_in.at[0 : n_y - 1], table_sem)
+
     sums = []
     for h in range(2):
-        wait_bytes(part.at[h, 0 : n_y - 1], part_sem.at[h])
-        whole = part[h, 0]
+        wait_bytes(part.at[0 : n_y - 1], part_sem.at[h])
+        whole = part[h * n_y]
         for k in range(1, n_y):
-            whole = whole + part[h, k]
+            whole = whole + part[h * n_y + k]
         sums.append(whole)
     left, right_ = sums[0], sums[1]
     all_sum = jnp.concatenate(
@@ -334,14 +342,7 @@
         block_sum = jnp.sum(jnp.where(row_id < count, block, 0.0), axis=0, keepdims=True)
         exc_ref[b : b + 1, :] = block_sum / count.astype(f32) - global_mean
 
-    wait_bytes(heard, note_send)
-    for h in range(2):
-        wait_bytes(rows_in.at[h, 0, 0 : n_lat - 1], rows_send.at[h, 0])
-        wait_bytes(rows_in.at[h, 1], rows_send.at[h, 1])
-        wait_bytes(part.at[h, 0 : n_y - 1], part_send.at[h])
-    wait_bytes(near_in.at[0 : PAIR * SUB - 1], sum_send.at[0])
-    wait_bytes(mid_in.at[0 : n_z - 1], sum_send.at[1])
-    wait_bytes(far_in.at[0 : n_y - 1], sum_send.at[2])
+    wait_bytes(part.at[0 : 2 * (n_y - 1)], note_send)
 
 
 def put_out(stat_ref, exc_ref, stat_out, exc_out, stat_sem, exc_sem):
@@ -378,30 +379,28 @@
         scratch_shapes=[
             pltpu.VMEM((bins, width), jnp.bfloat16),
             pltpu.SMEM((blocks,), jnp.int32),
-            pltpu.VMEM((2, points), jnp.int32),
-            pltpu.VMEM((n_z, SUB, 2, points), jnp.int32),
-            pltpu.VMEM((2, points), jnp.int32),
+            pltpu.VMEM((3, points), jnp.int32),
+            pltpu.VMEM((n_z, SUB, 3, points), jnp.int32),
+            pltpu.VMEM((3, points), jnp.int32),
             pltpu.VMEM((2, n_z, SUB, slots // 2, width), jnp.float32),
-            pltpu.VMEM((2, PAIR, n_lat, slots // 2, width), jnp.float32),
+            pltpu.VMEM((2 * PAIR * n_lat, slots // 2, width), jnp.float32),
             pltpu.VMEM((3, 1, width), jnp.float32),
             pltpu.VMEM((PAIR * SUB, 1, width), jnp.float32),
             pltpu.VMEM((n_z, 1, width), jnp.float32),
             pltpu.VMEM((n_y, 1, width), jnp.float32),
-            pltpu.VMEM((PAIR, 2 * points, n_lat * slots // 2), jnp.bfloat16),
-            pltpu.VMEM((2, n_y, points // 2, width), jnp.float32),
+            pltpu.VMEM((PAIR, 2 * points, n_lat * slots), jnp.bfloat16),
+            pltpu.VMEM((2 * n_y, points // 2, width), jnp.float32),
             dma,
             dma,
             dma,
             dma,
             dma((n_z // 2 + 1,)),
             dma,
-            dma((2, 2)),
+            dma,
             dma((2, PAIR)),
-            dma((3,)),
-            dma,
-            dma,
-            dma,
-            dma((2,)),
+            dma,
+            dma,
+            dma,
             dma((2,)),
         ],
         compiler_params=pltpu.CompilerParams(collective_id=0, has_side_effects=True),

time: 30.1 us -> 29.9 us (level)
  no operation moved by 1% of the time
where the time goes in v7:
time: 29.9 us; the launch traced here: 29.8 us
  Pallas kernels  29.2 us (98%)
  between operations  0.64 us (2%)
    pallas_call x1, Pallas kernels, shards(): pl.pallas_call(functools.partial(kernel, n_seg, n_lat), out_shape=(pltpu....  28.5 us
    pallas_call x1, Pallas kernels, shards(): pl.pallas_call(put_out, out_shape=(jax.ShapeDtypeStruct((points, width),...  0.64 us

profile of v7, /device:TPU:1, one launch (start us, length us, event | category | flops | bytes accessed | tf_op | source)
XLA Modules:
  0.0 29.8 jit_solution(10397171681291928585)
XLA Ops:
  0.6 28.5 %shard_map.50 = (bf16[128,128]{1,0:T(8,128)(2,1)S(1)}, f32[2,128]{1,0:T(2,128)S(1)}) custom-call(bf16[1,2048,128]{2,1,0:T(8,128)(2,1)} %map_ref.1, s32[1,128]{1,0:T(1,128)} %pos_hbm.1, s32[2]{0:T(128)} %cnt_hbm.1), custom_call_target="tpu_custom_call" | custom-call | tf_op jit(solution)/shard_map/pallas_call | solution.py:367
  29.2 0.6 %shard_map.51 = (bf16[128,128]{1,0:T(8,128)(2,1)}, f32[2,128]{1,0:T(2,128)}) custom-call(bf16[128,128]{1,0:T(8,128)(2,1)S(1)} %get-tuple-element.4.stat_ref, f32[2,128]{1,0:T(2,128)S(1)} %get-tuple-element.5.exc_ref), custom_call_target="tpu_custom_call" | custom-call | tf_op jit(solution)/shard_map/pallas_call | solution.py:409

commit v8 on v7

--- a/solution.py
+++ b/solution.py
@@ -186,7 +186,7 @@
                 rows_sem.at[h, group],
             ).start()
 
-    order = [[], [((1, 2), 0, ""), ((1, 2), 1, "e")], [((3, 4), 0, "")], [((5, 6), 0, "e")], [((7,), 0, "e"), ((5, 6, 7), 1, "e"), ((3, 4), 1, "e"), ((5, 6, 7), 0, "l"), ((5, 6, 7, 3, 4, 1, 2), 1, "l")]]
+    order = [[], [((1, 2), 0, ""), ((1, 2), 1, "e")], [((3, 4), 0, "")], [((5, 6), 0, "e")], [((7,), 0, "e"), ((7, 5, 6), 1, "e"), ((3, 4), 1, "e"), ((7, 5, 6), 0, "l"), ((7, 5, 6, 3, 4, 1, 2), 1, "l")]]
     early = [first_at[i] < half * SUB for i in range(n_z)]
 
     tile = (1, slots, width)
@@ -227,6 +227,18 @@
         total_sum += jnp.sum(jnp.where(is_valid, rows, 0.0), axis=0, keepdims=True)
         total_count += jnp.sum(valid, keepdims=True)
 
+        if k == 0:
+            give(0, 0)
+            give(0, 1)
+        for ids, h, cond in order[k]:
+            for i in ids:
+                if cond == "e":
+                    pl.when(early[i])(functools.partial(give, i, h))
+                elif cond == "l":
+                    pl.when(jnp.logical_not(early[i]))(functools.partial(give, i, h))
+                else:
+                    give(i, h)
+
         if k == len(waves) - 1:
             sum_out[0] = total_sum
             near_in[group * SUB + q] = total_sum
@@ -241,18 +253,6 @@
                     device_id=(g, d),
                     device_id_type=MESH,
                 ).start()
-
-        if k == 0:
-            give(0, 0)
-            give(0, 1)
-        for ids, h, cond in order[k]:
-            for i in ids:
-                if cond == "e":
-                    pl.when(early[i])(functools.partial(give, i, h))
-                elif cond == "l":
-                    pl.when(jnp.logical_not(early[i]))(functools.partial(give, i, h))
-                else:
-                    give(i, h)
 
     choose(other, pair_note[0:1, :])
 

time: 29.9 us -> 29.9 us (level)
  no operation moved by 1% of the time
where the time goes in v8:
time: 29.9 us; the launch traced here: 29.8 us
  Pallas kernels  29.2 us (98%)
  between operations  0.64 us (2%)
    pallas_call x1, Pallas kernels, shards(): pl.pallas_call(functools.partial(kernel, n_seg, n_lat), out_shape=(pltpu....  28.5 us
    pallas_call x1, Pallas kernels, shards(): pl.pallas_call(put_out, out_shape=(jax.ShapeDtypeStruct((points, width),...  0.64 us

profile of v8, /device:TPU:1, one launch (start us, length us, event | category | flops | bytes accessed | tf_op | source)
XLA Modules:
  0.0 29.8 jit_solution(15119831179614008630)
XLA Ops:
  0.6 28.5 %shard_map.50 = (bf16[128,128]{1,0:T(8,128)(2,1)S(1)}, f32[2,128]{1,0:T(2,128)S(1)}) custom-call(bf16[1,2048,128]{2,1,0:T(8,128)(2,1)} %map_ref.1, s32[1,128]{1,0:T(1,128)} %pos_hbm.1, s32[2]{0:T(128)} %cnt_hbm.1), custom_call_target="tpu_custom_call" | custom-call | tf_op jit(solution)/shard_map/pallas_call | solution.py:367
  29.2 0.6 %shard_map.51 = (bf16[128,128]{1,0:T(8,128)(2,1)}, f32[2,128]{1,0:T(2,128)}) custom-call(bf16[128,128]{1,0:T(8,128)(2,1)S(1)} %get-tuple-element.4.stat_ref, f32[2,128]{1,0:T(2,128)S(1)} %get-tuple-element.5.exc_ref), custom_call_target="tpu_custom_call" | custom-call | tf_op jit(solution)/shard_map/pallas_call | solution.py:409

commit v9 on v8

--- a/solution.py
+++ b/solution.py
@@ -73,8 +73,8 @@
 
     offsets = [0] + [o for k in range(1, half) for o in (k, n_z - k)] + [half]
     waves = [(0, 1)] + [(2 * k - 1, 2 * k + 1) for k in range(1, half)] + [(n_z - 1, n_z)]
-    first_at = [lax.rem(z + o, n_z) * SUB for o in offsets]
-    near_q = [lax.rem(q + s, SUB) for s in range(1, SUB)]
+    first_at = [lat - q + (o - jnp.where(z >= n_z - o, n_z, 0)) * SUB for o in offsets]
+    near_q = [q + s - jnp.where(q >= SUB - s, SUB, 0) for s in range(1, SUB)]
 
     def peers(i):
         if i == 0:

time: 29.9 us -> 29.9 us (level)
  no operation moved by 1% of the time
where the time goes in v9:
time: 29.9 us; the launch traced here: 29.8 us
  Pallas kernels  29.1 us (97%)
  between operations  0.64 us (2%)
    pallas_call x1, Pallas kernels, shards(): pl.pallas_call(functools.partial(kernel, n_seg, n_lat), out_shape=(pltpu....  28.5 us
    pallas_call x1, Pallas kernels, shards(): pl.pallas_call(put_out, out_shape=(jax.ShapeDtypeStruct((points, width),...  0.64 us

profile of v9, /device:TPU:1, one launch (start us, length us, event | category | flops | bytes accessed | tf_op | source)
XLA Modules:
  0.0 29.8 jit_solution(6915035605976223754)
XLA Ops:
  0.6 28.5 %shard_map.50 = (bf16[128,128]{1,0:T(8,128)(2,1)S(1)}, f32[2,128]{1,0:T(2,128)S(1)}) custom-call(bf16[1,2048,128]{2,1,0:T(8,128)(2,1)} %map_ref.1, s32[1,128]{1,0:T(1,128)} %pos_hbm.1, s32[2]{0:T(128)} %cnt_hbm.1), custom_call_target="tpu_custom_call" | custom-call | tf_op jit(solution)/shard_map/pallas_call | solution.py:367
  29.1 0.6 %shard_map.51 = (bf16[128,128]{1,0:T(8,128)(2,1)}, f32[2,128]{1,0:T(2,128)}) custom-call(bf16[128,128]{1,0:T(8,128)(2,1)S(1)} %get-tuple-element.4.stat_ref, f32[2,128]{1,0:T(2,128)S(1)} %get-tuple-element.5.exc_ref), custom_call_target="tpu_custom_call" | custom-call | tf_op jit(solution)/shard_map/pallas_call | solution.py:409

commit v10 on v9

--- a/solution.py
+++ b/solution.py
@@ -79,7 +79,7 @@
     def peers(i):
         if i == 0:
             return [(nq, first_at[0] + nq) for nq in near_q]
-        return [(s, first_at[i] + s) for s in (1, 3, 2, 0)]
+        return [(s, first_at[i] + s) for s in (1, 0, 3, 2)]
 
     y_peers = [group * n_y + k + jnp.where(y <= k, 1, 0) for k in range(n_y - 1)]
     far_first = list(range(n_z - 1, -1, -1))

time: 29.9 us -> 29.7 us (level)
  no operation moved by 1% of the time
where the time goes in v10:
time: 29.7 us; the launch traced here: 29.6 us
  Pallas kernels  29 us (98%)
  between operations  0.64 us (2%)
    pallas_call x1, Pallas kernels, shards(): pl.pallas_call(functools.partial(kernel, n_seg, n_lat), out_shape=(pltpu....  28.3 us
    pallas_call x1, Pallas kernels, shards(): pl.pallas_call(put_out, out_shape=(jax.ShapeDtypeStruct((points, width),...  0.64 us

profile of v10, /device:TPU:1, one launch (start us, length us, event | category | flops | bytes accessed | tf_op | source)
XLA Modules:
  0.0 29.6 jit_solution(1221098853640809223)
XLA Ops:
  0.6 28.3 %shard_map.50 = (bf16[128,128]{1,0:T(8,128)(2,1)S(1)}, f32[2,128]{1,0:T(2,128)S(1)}) custom-call(bf16[1,2048,128]{2,1,0:T(8,128)(2,1)} %map_ref.1, s32[1,128]{1,0:T(1,128)} %pos_hbm.1, s32[2]{0:T(128)} %cnt_hbm.1), custom_call_target="tpu_custom_call" | custom-call | tf_op jit(solution)/shard_map/pallas_call | solution.py:367
  29.0 0.6 %shard_map.51 = (bf16[128,128]{1,0:T(8,128)(2,1)}, f32[2,128]{1,0:T(2,128)}) custom-call(bf16[128,128]{1,0:T(8,128)(2,1)S(1)} %get-tuple-element.4.stat_ref, f32[2,128]{1,0:T(2,128)S(1)} %get-tuple-element.5.exc_ref), custom_call_target="tpu_custom_call" | custom-call | tf_op jit(solution)/shard_map/pallas_call | solution.py:409
